TPU v7x, 32 devices: a whole 2x2x4 slice. The times are simulated.
32 devices in a mesh: pp: 4 (over z), tp: 4 (over y, core), ep: 2 (over x).
Axes of the slice: x: 2, y: 2, z: 4, core: 2. Of those that a mesh axis runs over, the one named last changes fastest.
Arguments:
- incoming: bfloat16 [4, 1024, 2048], P('pp', ('tp', 'ep')), may hold values from -6 to 6
- expert_ids: int32 [4, 1024, 2], P('pp', ('tp', 'ep')), may hold values from 0 to 7, all different within a row; in each aligned block of 128 rows (0 to 127, 128 to 255, ..., all dimensions but the last counted through in order) at most 64 rows name the same one
- gate_scores: float32 [4, 1024, 2], P('pp', ('tp', 'ep')), may hold values from 0.05 to 1
- gate_proj: bfloat16 [8, 2048, 768], P(('tp', 'ep')), may hold values from -0.125 to 0.125
- up_proj: bfloat16 [8, 2048, 768], P(('tp', 'ep')), may hold values from -0.125 to 0.125
- down_proj: bfloat16 [8, 768, 2048], P(('tp', 'ep')), may hold values from -0.21875 to 0.21875
Outputs:
- combined: bfloat16 [4, 1024, 2048], P('pp', ('tp', 'ep'))
Inputs may be any that keep to these rules, and one draw needn't show every extreme that they name: `expert_ids`: each token names 2 different experts. Among the tokens of one device of one section no expert is named more than 64 times, and in every draw some device's tokens name one expert exactly 64 times.
All inputs are finite; a program needn't handle non-finite values.
Results may differ from a plain program's by a relative error of at most 0.0045.
Values may be sent and summed in bfloat16 or wider, within the bound.
A program may use at most 64 MiB of HBM per device.

v0:
```python
import functools

import jax
import jax.numpy as jnp
from jax import lax
from jax.experimental import pallas as pl
from jax.experimental.pallas import tpu as pltpu
from jax.sharding import PartitionSpec as P

MESH = pl.DeviceIdType.MESH
OWN, ACROSS_X, ACROSS_Y, DIAGONAL = range(4)


def shifted(block, axis, distance):
    devices = range(lax.axis_size(axis))
    route = [((i - distance) % len(devices), i) for i in devices]
    return lax.ppermute(block, axis, route)


def expert_apply(tokens_in, gate_mat, up_mat, down_mat):
    gate_part = jnp.dot(tokens_in, gate_mat, preferred_element_type=jnp.float32)
    upward = jnp.dot(tokens_in, up_mat, preferred_element_type=jnp.float32)
    hidden = (jax.nn.silu(gate_part) * upward).astype(jnp.bfloat16)
    return jnp.dot(hidden, down_mat, preferred_element_type=jnp.float32).astype(jnp.bfloat16)


def shards(incoming, expert_ids, gate_scores, gate_proj, up_proj, down_proj):
    arrived = shifted(incoming, "pp", 1)[0]
    tok_count, features = arrived.shape
    top_count = expert_ids.shape[2]
    expert_count = lax.axis_size("tp") * lax.axis_size("ep")
    capacity = min(tok_count, 2 * tok_count * top_count // expert_count)
    values = arrived.astype(jnp.float32)
    normed = (values * lax.rsqrt(jnp.mean(values * values, axis=1, keepdims=True) + 1e-06)).astype(
        jnp.bfloat16
    )
    chosen = expert_ids[0].reshape(-1)
    onehot = (chosen[:, None] == jnp.arange(expert_count, dtype=jnp.int32)[None, :]).astype(
        jnp.int32
    )
    before = jnp.cumsum(onehot, axis=0) - onehot
    slot_of = jnp.sum(before * onehot, axis=1)
    destination = chosen * capacity + slot_of
    owner_row = jnp.arange(chosen.shape[0], dtype=jnp.int32) // top_count
    source_row = (
        jnp.full((expert_count * capacity,), tok_count, jnp.int32).at[destination].set(owner_row)
    )
    occupied = jnp.zeros((expert_count * capacity,), jnp.int32).at[destination].set(1)
    with_blank = jnp.concatenate([normed, jnp.zeros((1, features), jnp.bfloat16)], axis=0)
    outgoing = with_blank[source_row].reshape(expert_count, capacity, features)
    occupied = occupied.reshape(expert_count, capacity)
    gate_mat, up_mat, down_mat = (gate_proj[0], up_proj[0], down_proj[0])
    received_rows = lax.all_to_all(outgoing, ("tp", "ep"), split_axis=0, concat_axis=0, tiled=True)
    flat_rows = received_rows.reshape(-1, features)
    flat_live = lax.all_to_all(
        occupied, ("tp", "ep"), split_axis=0, concat_axis=0, tiled=True
    ).reshape(-1)
    answered = expert_apply(flat_rows, gate_mat, up_mat, down_mat) * flat_live[:, None].astype(
        jnp.bfloat16
    )
    answered = answered.reshape(received_rows.shape)
    returned = lax.all_to_all(answered, ("tp", "ep"), split_axis=0, concat_axis=0, tiled=True)
    picked = returned.reshape(expert_count * capacity, features)[destination].reshape(
        tok_count, top_count, features
    )
    scores = gate_scores[0]
    weights = scores / jnp.sum(scores, axis=1, keepdims=True)
    combined = values + jnp.sum(weights[:, :, None] * picked.astype(jnp.float32), axis=1)
    return combined.astype(jnp.bfloat16)[None]


def exchange_kernel(
    sizes,
    incoming,
    ids_hbm,
    scores_hbm,
    gate_hbm,
    up_hbm,
    down_hbm,
    out_ref,
    gate_w,
    up_w,
    down_w,
    tok,
    meta_ids,
    meta_scores,
    packed,
    hidden,
    kept,
    passed,
    partner,
    to_x,
    to_y,
    to_d,
    from_x,
    from_y,
    via_x,
    via_y,
    total,
    send_sem,
    recv_sem,
    load_sem,
):
    n_pp, n_tp, n_ep, top, cap, chunks, pieces = sizes
    rows, features = tok.shape[2:]
    ff = hidden.shape[1]
    pp, tp, ep = lax.axis_index("pp"), lax.axis_index("tp"), lax.axis_index("ep")
    other_core = tp + 1 - 2 * (tp % 2)
    at_x = {"ep": (ep + 1) % n_ep}
    at_y = {"tp": (tp + 2) % n_tp}
    at_core = {"tp": other_core}
    ahead, behind = {"pp": (pp + 1) % n_pp}, {"pp": (pp + n_pp - 1) % n_pp}

    splits = 3 * chunks
    loads = []
    for src, dst in ((gate_hbm, gate_w), (up_hbm, up_w), (down_hbm, down_w)):
        depth = dst.shape[0] // chunks
        for c in range(chunks):
            cut = pl.ds(c * depth, depth)
            loads.append(pltpu.make_async_copy(src.at[0, cut], dst.at[cut], load_sem.at[len(loads)]))
    own_meta = [
        pltpu.make_async_copy(ids_hbm, meta_ids.at[0], load_sem.at[splits]),
        pltpu.make_async_copy(scores_hbm, meta_scores.at[0], load_sem.at[splits + 1]),
    ]

    barrier = pltpu.get_barrier_semaphore()
    for peer in (at_x, at_y, at_core, ahead, behind):
        pl.semaphore_signal(barrier, inc=1, device_id=peer, device_id_type=MESH)
    for copy in own_meta:
        copy.start()
    pl.semaphore_wait(barrier, 5)

    started = []

    def link(src, dst, peer):
        i = len(started)
        copy = pltpu.make_async_remote_copy(
            src_ref=src,
            dst_ref=dst,
            send_sem=send_sem.at[i],
            recv_sem=recv_sem.at[i],
            device_id=peer,
            device_id_type=MESH,
        )
        started.append(copy)
        copy.start()
        return copy

    size = rows // chunks
    part = [pl.ds(c * size, size) for c in range(chunks)]

    def block(role, side, c):
        return tok.at[role, side, part[c]]

    hop = [link(incoming.at[0, part[c]], block(OWN, 0, c), ahead) for c in range(chunks)]
    for copy in own_meta:
        copy.wait()

    def meta_link(src, dst, peer):
        return [link(m.at[src], m.at[dst], peer) for m in (meta_ids, meta_scores)]

    meta_x = meta_link(0, 2, at_x)
    meta_y = meta_link(0, 4, at_y)
    meta_core = meta_link(0, 1, at_core)
    out_x, out_y, out_d, core = {}, {}, {}, {}

    def relay(c):
        out_x[c].wait_recv()
        if c % 2 == 0:
            out_d[c] = link(block(ACROSS_X, 0, c), block(DIAGONAL, 0, c), at_y)
        core[ACROSS_X, c] = link(block(ACROSS_X, 0, c), block(ACROSS_X, 1, c), at_core)
        out_y[c].wait_recv()
        if c % 2 == 1:
            out_d[c] = link(block(ACROSS_Y, 0, c), block(DIAGONAL, 0, c), at_x)
        core[ACROSS_Y, c] = link(block(ACROSS_Y, 0, c), block(ACROSS_Y, 1, c), at_core)

    def relay_diagonal(c):
        out_d[c].wait_recv()
        core[DIAGONAL, c] = link(block(DIAGONAL, 0, c), block(DIAGONAL, 1, c), at_core)

    lag = chunks
    for c in range(chunks):
        hop[c].wait_recv()
        out_x[c] = link(block(OWN, 0, c), block(ACROSS_X, 0, c), at_x)
        out_y[c] = link(block(OWN, 0, c), block(ACROSS_Y, 0, c), at_y)
        core[OWN, c] = link(block(OWN, 0, c), block(OWN, 1, c), at_core)
        if c == 0:
            for copy in meta_x:
                copy.wait_recv()
            meta_d = meta_link(2, 6, at_y)
            meta_core += meta_link(2, 3, at_core)
            for copy in meta_y:
                copy.wait_recv()
            meta_core += meta_link(4, 5, at_core)
        if c == chunks // 2:
            for copy in meta_d:
                copy.wait_recv()
            meta_core += meta_link(6, 7, at_core)
        for copy in loads[c::chunks]:
            copy.start()
        if c >= lag:
            relay(c - lag)
    for copy in meta_core:
        copy.wait_recv()

    lane = lax.broadcasted_iota(jnp.int32, (rows, rows), 1)
    earlier = (lax.broadcasted_iota(jnp.int32, (rows, rows), 0) < lane).astype(jnp.bfloat16)
    ids = [meta_ids[:, k, :] for k in range(top)]
    scores = [meta_scores[:, k, :] for k in range(top)]
    score_sum = functools.reduce(jnp.add, scores)

    def ranks(expert):
        named = [i == expert for i in ids]
        any_named = functools.reduce(jnp.logical_or, named)
        before = jnp.dot(
            any_named.astype(jnp.float32).astype(jnp.bfloat16),
            earlier,
            preferred_element_type=jnp.float32,
        )
        score = sum(jnp.where(n, s, 0.0) for n, s in zip(named, scores))
        return jnp.where(any_named, before, -1.0), score / score_sum

    mine = tp * n_ep + ep
    theirs = other_core * n_ep + ep
    slot_mine, weight_mine = ranks(mine)
    slot_theirs, _ = ranks(theirs)
    slot_index = lax.broadcasted_iota(jnp.int32, (cap, rows), 0).astype(jnp.float32)

    def slots(rank, i):
        return slot_index == rank[i : i + 1, :]

    def pack(role):
        for side in range(2):
            pick = slots(slot_mine, 2 * role + side)
            chosen = jnp.dot(
                pick.astype(jnp.float32).astype(jnp.bfloat16),
                tok[role, side],
                preferred_element_type=jnp.float32,
            )
            scale = lax.rsqrt(jnp.mean(chosen * chosen, axis=1, keepdims=True) + 1e-06)
            packed[role, pl.ds(side * cap, cap)] = (chosen * scale).astype(jnp.bfloat16)

    def expert(role):
        step = 256 if ff % 256 == 0 else 128
        tokens_in = packed[role]
        for n in range(ff // step):
            cols = pl.ds(n * step, step)
            gate = jnp.dot(tokens_in, gate_w[:, cols], preferred_element_type=jnp.float32)
            upward = jnp.dot(tokens_in, up_w[:, cols], preferred_element_type=jnp.float32)
            hidden[:, cols] = (gate / (1.0 + jnp.exp(-gate)) * upward).astype(jnp.bfloat16)
        weight = [
            jnp.sum(
                jnp.where(slots(slot_mine, 2 * role + side), weight_mine[2 * role + side :][:1], 0.0),
                axis=1,
                keepdims=True,
            )
            for side in range(2)
        ]
        inner = hidden[...]
        for n in range(features // 256):
            cols = pl.ds(n * 256, 256)
            y = jnp.dot(inner, down_w[:, cols], preferred_element_type=jnp.float32)
            y = y.astype(jnp.bfloat16).astype(jnp.float32)
            kept[role, :, cols] = (y[:cap] * weight[0]).astype(jnp.bfloat16)
            passed[role, :, cols] = (y[cap:] * weight[1]).astype(jnp.bfloat16)
        return link(passed.at[role], partner.at[role], at_core)

    def spread(role):
        both = jnp.concatenate(
            [slots(slot_mine, 2 * role), slots(slot_theirs, 2 * role)], axis=0
        ).astype(jnp.float32)
        return both.T.astype(jnp.bfloat16)

    def unpack(role, matrix, lo, hi):
        values = jnp.concatenate([kept[role], partner[role]], axis=0)
        return jnp.dot(matrix[lo:hi], values, preferred_element_type=jnp.float32)

    half = rows // 2
    piece = half // pieces
    cuts = [(p * piece, (p + 1) * piece) for p in range(pieces)]
    for c in range(chunks - lag, chunks):
        relay(c)
    for role in (ACROSS_X, ACROSS_Y):
        for c in range(chunks):
            core[role, c].wait_recv()
    pack(ACROSS_X)
    pack(ACROSS_Y)
    for copy in loads:
        copy.wait()
    swap = {ACROSS_X: expert(ACROSS_X)}
    swap[ACROSS_Y] = expert(ACROSS_Y)
    for c in range(chunks):
        relay_diagonal(c)

    last_x, last_y, last_d = [], [], []

    def post(buffer, landing, lo, hi, value, peer, sends):
        buffer[lo:hi] = value.astype(jnp.bfloat16)
        sends.append(link(buffer.at[pl.ds(lo, hi - lo)], landing, peer))

    swap[ACROSS_X].wait_recv()
    spread_x = spread(ACROSS_X)
    for lo, hi in cuts:
        land = from_x.at[pl.ds(lo, piece)]
        post(to_x, land, lo, hi, unpack(ACROSS_X, spread_x, lo, hi), at_x, last_x)
    swap[ACROSS_Y].wait_recv()
    spread_y = spread(ACROSS_Y)
    for lo, hi in cuts:
        lo, hi = lo + half, hi + half
        land = from_y.at[pl.ds(lo, piece)]
        post(to_y, land, lo, hi, unpack(ACROSS_Y, spread_y, lo, hi), at_y, last_y)
    for c in range(chunks):
        core[DIAGONAL, c].wait_recv()
    pack(DIAGONAL)
    swap[DIAGONAL] = expert(DIAGONAL)
    for c in range(chunks):
        core[OWN, c].wait_recv()
    pack(OWN)
    swap[DIAGONAL].wait_recv()
    spread_d = spread(DIAGONAL)
    over_x, over_y = [], []
    for lo, hi in cuts:
        land = via_x.at[pl.ds(lo, piece)]
        post(to_d, land, lo, hi, unpack(DIAGONAL, spread_d, lo, hi), at_x, over_x)
        land = via_y.at[pl.ds(lo, piece)]
        lo, hi = lo + half, hi + half
        post(to_d, land, lo, hi, unpack(DIAGONAL, spread_d, lo, hi), at_y, over_y)
    swap[OWN] = expert(OWN)
    for p, (lo, hi) in enumerate(cuts):
        over_x[p].wait_recv()
        added = via_x[lo:hi].astype(jnp.float32)
        land = from_y.at[pl.ds(lo, piece)]
        post(to_y, land, lo, hi, unpack(ACROSS_Y, spread_y, lo, hi) + added, at_y, last_y)
        over_y[p].wait_recv()
        added = via_y[lo:hi].astype(jnp.float32)
        lo, hi = lo + half, hi + half
        land = from_x.at[pl.ds(lo, piece)]
        post(to_x, land, lo, hi, unpack(ACROSS_X, spread_x, lo, hi) + added, at_x, last_x)
    swap[OWN].wait_recv()
    total[...] = unpack(OWN, spread(OWN), 0, rows) + tok[OWN, 0].astype(jnp.float32)
    for p, (lo, hi) in enumerate(cuts):
        last_x[p].wait_recv()
        total[lo:hi] += from_x[lo:hi].astype(jnp.float32)
        last_y[p].wait_recv()
        total[lo + half : hi + half] += from_y[lo + half : hi + half].astype(jnp.float32)
    for p, (lo, hi) in enumerate(cuts):
        last_y[pieces + p].wait_recv()
        done = total[lo:hi] + from_y[lo:hi].astype(jnp.float32)
        out_ref[0, lo:hi] = done.astype(jnp.bfloat16)
        last_x[pieces + p].wait_recv()
        lo, hi = lo + half, hi + half
        done = total[lo:hi] + from_x[lo:hi].astype(jnp.float32)
        out_ref[0, lo:hi] = done.astype(jnp.bfloat16)
    for copy in started:
        copy.wait_send()


def fused(incoming, expert_ids, gate_scores, gate_proj, up_proj, down_proj):
    _, rows, features = incoming.shape
    top, ff = expert_ids.shape[2], gate_proj.shape[2]
    n_pp, n_tp, n_ep = (lax.axis_size(a) for a in ("pp", "tp", "ep"))
    cap = min(rows, 2 * rows * top // (n_tp * n_ep))
    chunks, pieces = 8, 2
    hbm, vmem = pl.BlockSpec(memory_space=pl.ANY), pl.BlockSpec(memory_space=pltpu.VMEM)
    narrow = functools.partial(pltpu.VMEM, dtype=jnp.bfloat16)
    copies = 8 * chunks + 2 * 7 + 4 + 6 * pieces
    return pl.pallas_call(
        functools.partial(exchange_kernel, (n_pp, n_tp, n_ep, top, cap, chunks, pieces)),
        out_shape=pltpu.VMEM(incoming.shape, incoming.dtype),
        in_specs=[hbm] * 6,
        out_specs=vmem,
        scratch_shapes=[
            narrow((features, ff)),
            narrow((features, ff)),
            narrow((ff, features)),
            narrow((4, 2, rows, features)),
            pltpu.VMEM((8, top, rows), jnp.int32),
            pltpu.VMEM((8, top, rows), jnp.float32),
            narrow((4, 2 * cap, features)),
            narrow((2 * cap, ff)),
            narrow((4, cap, features)),
            narrow((4, cap, features)),
            narrow((4, cap, features)),
            narrow((rows, features)),
            narrow((rows, features)),
            narrow((rows, features)),
            narrow((rows, features)),
            narrow((rows, features)),
            narrow((rows // 2, features)),
            narrow((rows // 2, features)),
            pltpu.VMEM((rows, features), jnp.float32),
            pltpu.SemaphoreType.DMA((copies,)),
            pltpu.SemaphoreType.DMA((copies,)),
            pltpu.SemaphoreType.DMA((3 * chunks + 2,)),
        ],
        compiler_params=pltpu.CompilerParams(collective_id=0, has_side_effects=True),
    )(incoming, expert_ids[0].T, gate_scores[0].T, gate_proj, up_proj, down_proj)


def solution(mesh):
    placed = (
        P("pp", ("tp", "ep"), None),
        P("pp", ("tp", "ep"), None),
        P("pp", ("tp", "ep"), None),
        P(("tp", "ep"), None, None),
        P(("tp", "ep"), None, None),
        P(("tp", "ep"), None, None),
    )
    square = mesh.shape["tp"] == 4 and mesh.shape["ep"] == 2 and mesh.shape["pp"] > 1
    return jax.shard_map(
        fused if square else shards,
        mesh=mesh,
        in_specs=placed,
        out_specs=P("pp", ("tp", "ep"), None),
        check_vma=False,
    )
```

profile of v0, /device:TPU:0, one launch (start us, length us, event | category | flops | bytes accessed | tf_op | source)
XLA Modules:
  0.0 50.9 jit_solution(15933087454570634944)
XLA Ops:
  0.0 50.1 %shard_map.64 = bf16[1,128,2048]{2,1,0:T(8,128)(2,1)S(1)} custom-call(bf16[1,128,2048]{2,1,0:T(8,128)(2,1)} %incoming.1, s32[2,128]{1,0:T(2,128)} %bitcast.6, f32[2,128]{1,0:T(2,128)} %bitcast.7, bf16[1,2048,768]{2,1,0:T(8,128)(2,1)} %gate_hbm.1, bf16[1,2048,768]{2,1,0:T(8,128)(2,1)} %up_hbm.1, bf16[1,768,2048]{2,1,0:T(8,128)(2,1)} %down_hbm.1), custom_call_target="tpu_custom_call" | custom-call | tf_op jit(solution)/shard_map/pallas_call | solution.py:367
  50.1 0.8 %copy.8 = bf16[1,128,2048]{2,1,0:T(8,128)(2,1)} copy(bf16[1,128,2048]{2,1,0:T(8,128)(2,1)S(1)} %shard_map.64) | data formatting | bytes 1048576
where the time goes:
time: 51 us; the launch traced here: 50.9 us
  Pallas kernels  50.1 us (98%)
  local copies, waits for them, and re-layouts  0.8 us (2%)
    pallas_call x1, Pallas kernels, fused(): pl.pallas_call(functools.partial(exchange_kernel, (n_pp, n_tp, n_ep, top,...  50.1 us

commit v1 on v0

v1 whole, which is shorter than its diff:
```python
import functools

import jax
import jax.numpy as jnp
from jax import lax
from jax.experimental import pallas as pl
from jax.experimental.pallas import tpu as pltpu
from jax.sharding import PartitionSpec as P

MESH = pl.DeviceIdType.MESH
OWN, ACROSS_X, ACROSS_Y, DIAGONAL = range(4)
EARLY, LATE = range(2)


def shifted(block, axis, distance):
    devices = range(lax.axis_size(axis))
    route = [((i - distance) % len(devices), i) for i in devices]
    return lax.ppermute(block, axis, route)


def expert_apply(tokens_in, gate_mat, up_mat, down_mat):
    gate_part = jnp.dot(tokens_in, gate_mat, preferred_element_type=jnp.float32)
    upward = jnp.dot(tokens_in, up_mat, preferred_element_type=jnp.float32)
    hidden = (jax.nn.silu(gate_part) * upward).astype(jnp.bfloat16)
    return jnp.dot(hidden, down_mat, preferred_element_type=jnp.float32).astype(jnp.bfloat16)


def shards(incoming, expert_ids, gate_scores, gate_proj, up_proj, down_proj):
    arrived = shifted(incoming, "pp", 1)[0]
    tok_count, features = arrived.shape
    top_count = expert_ids.shape[2]
    expert_count = lax.axis_size("tp") * lax.axis_size("ep")
    capacity = min(tok_count, 2 * tok_count * top_count // expert_count)
    values = arrived.astype(jnp.float32)
    normed = (values * lax.rsqrt(jnp.mean(values * values, axis=1, keepdims=True) + 1e-06)).astype(
        jnp.bfloat16
    )
    chosen = expert_ids[0].reshape(-1)
    onehot = (chosen[:, None] == jnp.arange(expert_count, dtype=jnp.int32)[None, :]).astype(
        jnp.int32
    )
    before = jnp.cumsum(onehot, axis=0) - onehot
    slot_of = jnp.sum(before * onehot, axis=1)
    destination = chosen * capacity + slot_of
    owner_row = jnp.arange(chosen.shape[0], dtype=jnp.int32) // top_count
    source_row = (
        jnp.full((expert_count * capacity,), tok_count, jnp.int32).at[destination].set(owner_row)
    )
    occupied = jnp.zeros((expert_count * capacity,), jnp.int32).at[destination].set(1)
    with_blank = jnp.concatenate([normed, jnp.zeros((1, features), jnp.bfloat16)], axis=0)
    outgoing = with_blank[source_row].reshape(expert_count, capacity, features)
    occupied = occupied.reshape(expert_count, capacity)
    gate_mat, up_mat, down_mat = (gate_proj[0], up_proj[0], down_proj[0])
    received_rows = lax.all_to_all(outgoing, ("tp", "ep"), split_axis=0, concat_axis=0, tiled=True)
    flat_rows = received_rows.reshape(-1, features)
    flat_live = lax.all_to_all(
        occupied, ("tp", "ep"), split_axis=0, concat_axis=0, tiled=True
    ).reshape(-1)
    answered = expert_apply(flat_rows, gate_mat, up_mat, down_mat) * flat_live[:, None].astype(
        jnp.bfloat16
    )
    answered = answered.reshape(received_rows.shape)
    returned = lax.all_to_all(answered, ("tp", "ep"), split_axis=0, concat_axis=0, tiled=True)
    picked = returned.reshape(expert_count * capacity, features)[destination].reshape(
        tok_count, top_count, features
    )
    scores = gate_scores[0]
    weights = scores / jnp.sum(scores, axis=1, keepdims=True)
    combined = values + jnp.sum(weights[:, :, None] * picked.astype(jnp.float32), axis=1)
    return combined.astype(jnp.bfloat16)[None]


def exchange_kernel(
    sizes,
    incoming,
    ids_hbm,
    scores_hbm,
    gate_hbm,
    up_hbm,
    down_hbm,
    out_ref,
    gate_w,
    up_w,
    down_w,
    tok_early,
    tok_late,
    meta_ids,
    meta_scores,
    hidden,
    kept_early,
    kept_late,
    passed_early,
    passed_late,
    partner_early,
    partner_late,
    to_early,
    to_late,
    from_early,
    from_late,
    via_early,
    via_late,
    done_early,
    send_sem,
    recv_sem,
    load_sem,
):
    n_pp, n_tp, n_ep, top, chunks, pieces = sizes
    features, ff = gate_w.shape
    pp, tp, ep = lax.axis_index("pp"), lax.axis_index("tp"), lax.axis_index("ep")
    other_core = tp + 1 - 2 * (tp % 2)
    at_x = {"ep": (ep + 1) % n_ep}
    at_y = {"tp": (tp + 2) % n_tp}
    at_core = {"tp": other_core}
    ahead, behind = {"pp": (pp + 1) % n_pp}, {"pp": (pp + n_pp - 1) % n_pp}

    tok = (tok_early, tok_late)
    kept, passed = (kept_early, kept_late), (passed_early, passed_late)
    partner = (partner_early, partner_late)
    to, landed, via = (to_early, to_late), (from_early, from_late), (via_early, via_late)
    count = [t.shape[2] for t in tok]
    first_row = [count[LATE], 0]
    half = [n // 2 for n in count]
    part = [[pl.ds(c * (n // m), n // m) for c in range(m)] for n, m in zip(count, chunks)]

    loads = []
    for src, dst in ((gate_hbm, gate_w), (up_hbm, up_w), (down_hbm, down_w)):
        loads.append(pltpu.make_async_copy(src.at[0], dst, load_sem.at[len(loads)]))
    own_rows = pltpu.make_async_copy(
        incoming.at[0, pl.ds(first_row[EARLY], count[EARLY])], tok_early.at[OWN, 0], load_sem.at[3]
    )
    own_meta = [
        pltpu.make_async_copy(ids_hbm, meta_ids.at[0, LATE], load_sem.at[4]),
        pltpu.make_async_copy(scores_hbm, meta_scores.at[0, LATE], load_sem.at[5]),
    ]

    barrier = pltpu.get_barrier_semaphore()
    for peer in (at_x, at_y, at_core, ahead, behind):
        pl.semaphore_signal(barrier, inc=1, device_id=peer, device_id_type=MESH)
    own_rows.start()
    for copy in own_meta:
        copy.start()
    own_rows.wait()
    for copy in own_meta:
        copy.wait()
    pl.semaphore_wait(barrier, 5)

    started = []

    def link(src, dst, peer):
        i = len(started)
        copy = pltpu.make_async_remote_copy(
            src_ref=src,
            dst_ref=dst,
            send_sem=send_sem.at[i],
            recv_sem=recv_sem.at[i],
            device_id=peer,
            device_id_type=MESH,
        )
        started.append(copy)
        copy.start()
        return copy

    def block(g, role, side, c):
        return tok[g].at[role, side, part[g][c]]

    out_x, out_y, out_d, core = {}, {}, {}, {}

    def share(g, c):
        out_x[g, c] = link(block(g, OWN, 0, c), block(g, ACROSS_X, 0, c), at_x)
        out_y[g, c] = link(block(g, OWN, 0, c), block(g, ACROSS_Y, 0, c), at_y)
        core[g, OWN, c] = link(block(g, OWN, 0, c), block(g, OWN, 1, c), at_core)

    def relay(g, c):
        out_x[g, c].wait_recv()
        if c % 2 == 0:
            out_d[g, c] = link(block(g, ACROSS_X, 0, c), block(g, DIAGONAL, 0, c), at_y)
        core[g, ACROSS_X, c] = link(block(g, ACROSS_X, 0, c), block(g, ACROSS_X, 1, c), at_core)
        out_y[g, c].wait_recv()
        if c % 2 == 1:
            out_d[g, c] = link(block(g, ACROSS_Y, 0, c), block(g, DIAGONAL, 0, c), at_x)
        core[g, ACROSS_Y, c] = link(block(g, ACROSS_Y, 0, c), block(g, ACROSS_Y, 1, c), at_core)

    def relay_diagonal(g, c):
        out_d[g, c].wait_recv()
        core[g, DIAGONAL, c] = link(block(g, DIAGONAL, 0, c), block(g, DIAGONAL, 1, c), at_core)

    def meta_link(src, dst, peer):
        return [link(m.at[src], m.at[dst], peer) for m in (meta_ids, meta_scores)]

    def arrive(copies):
        for copy in copies:
            copy.wait_recv()

    mine = tp * n_ep + ep

    def weight(g, role):
        columns = []
        lane = lax.broadcasted_iota(jnp.int32, (count[g], meta_ids.shape[3]), 1)
        row = lax.broadcasted_iota(jnp.int32, (count[g], meta_ids.shape[3]), 0)
        for side in range(2):
            ids, scores = meta_ids[2 * role + side, g], meta_scores[2 * role + side, g]
            named = jnp.sum(jnp.where(ids == mine, scores, 0.0), axis=0, keepdims=True)
            share_of = named / jnp.sum(scores, axis=0, keepdims=True)
            columns.append(
                jnp.sum(jnp.where(lane == row + first_row[g], share_of, 0.0), axis=1, keepdims=True)
            )
        return columns

    swap = {}

    def expert(g, role):
        for c in range(chunks[g]):
            core[g, role, c].wait_recv()
        n = count[g]
        tokens_in = tok[g][role].reshape(2 * n, features)
        values = tokens_in.astype(jnp.float32)
        scale = lax.rsqrt(jnp.mean(values * values, axis=1, keepdims=True) + 1e-06)
        step = 256 if ff % 256 == 0 else 128
        for j in range(ff // step):
            cols = pl.ds(j * step, step)
            gate = jnp.dot(tokens_in, gate_w[:, cols], preferred_element_type=jnp.float32) * scale
            upward = jnp.dot(tokens_in, up_w[:, cols], preferred_element_type=jnp.float32) * scale
            hidden[: 2 * n, cols] = (gate / (1.0 + jnp.exp(-gate)) * upward).astype(jnp.bfloat16)
        inner = hidden[: 2 * n]
        here, there = weight(g, role)
        for j in range(features // 256):
            cols = pl.ds(j * 256, 256)
            y = jnp.dot(inner, down_w[:, cols], preferred_element_type=jnp.float32)
            y = y.astype(jnp.bfloat16).astype(jnp.float32)
            kept[g][role, :, cols] = (y[:n] * here).astype(jnp.bfloat16)
            passed[g][role, :, cols] = (y[n:] * there).astype(jnp.bfloat16)
        swap[g, role] = link(passed[g].at[role], partner[g].at[role], at_core)

    def summed(g, role, lo, hi):
        return kept[g][role, lo:hi].astype(jnp.float32) + partner[g][role, lo:hi].astype(jnp.float32)

    direct, merged, across = {}, {}, {}

    def cuts(g):
        size = half[g] // pieces
        return [(p * size, (p + 1) * size) for p in range(pieces)]

    def post(g, lane, landing, lo, hi, value, peer):
        to[g][lane, lo:hi] = value.astype(jnp.bfloat16)
        return link(to[g].at[lane, pl.ds(lo, hi - lo)], landing.at[pl.ds(lo, hi - lo)], peer)

    def send_diagonal(g):
        swap[g, DIAGONAL].wait_recv()
        for p, (lo, hi) in enumerate(cuts(g)):
            across[g, 0, p] = post(
                g, 2, via[g].at[0], lo, hi, summed(g, DIAGONAL, lo, hi), at_x
            )
            lo, hi = lo + half[g], hi + half[g]
            across[g, 1, p] = post(
                g, 2, via[g].at[0], lo, hi, summed(g, DIAGONAL, lo, hi), at_y
            )

    def send_direct(g):
        swap[g, ACROSS_X].wait_recv()
        for p, (lo, hi) in enumerate(cuts(g)):
            direct[g, 0, p] = post(g, 0, landed[g].at[0], lo, hi, summed(g, ACROSS_X, lo, hi), at_x)
        swap[g, ACROSS_Y].wait_recv()
        for p, (lo, hi) in enumerate(cuts(g)):
            lo, hi = lo + half[g], hi + half[g]
            direct[g, 1, p] = post(g, 1, landed[g].at[1], lo, hi, summed(g, ACROSS_Y, lo, hi), at_y)

    def send_merged(g):
        for p, (lo, hi) in enumerate(cuts(g)):
            across[g, 0, p].wait_recv()
            value = summed(g, ACROSS_Y, lo, hi) + via[g][0, lo:hi].astype(jnp.float32)
            merged[g, 0, p] = post(g, 1, landed[g].at[1], lo, hi, value, at_y)
            lo, hi = lo + half[g], hi + half[g]
            across[g, 1, p].wait_recv()
            value = summed(g, ACROSS_X, lo, hi) + via[g][0, lo:hi].astype(jnp.float32)
            merged[g, 1, p] = post(g, 0, landed[g].at[0], lo, hi, value, at_x)

    def finish(g):
        swap[g, OWN].wait_recv()
        for p, span in enumerate(cuts(g)):
            for k in range(2):
                lo, hi = (edge + k * half[g] for edge in span)
                value = summed(g, OWN, lo, hi) + tok[g][OWN, 0, lo:hi].astype(jnp.float32)
                direct[g, k, p].wait_recv()
                merged[g, k, p].wait_recv()
                value += landed[g][0, lo:hi].astype(jnp.float32)
                value += landed[g][1, lo:hi].astype(jnp.float32)
                value = value.astype(jnp.bfloat16)
                if g == LATE:
                    out_ref[0, lo:hi] = value
                else:
                    done_early[lo:hi] = value
                    cut = pl.ds(lo + first_row[g], hi - lo)
                    home.append(link(done_early.at[pl.ds(lo, hi - lo)], out_ref.at[0, cut], ahead))

    home = []
    hop = [
        link(incoming.at[0, part[LATE][c]], block(LATE, OWN, 0, c), ahead)
        for c in range(chunks[LATE])
    ]
    meta_early = [
        link(m.at[0, LATE], m.at[0, EARLY], behind) for m in (meta_ids, meta_scores)
    ]
    for c in range(chunks[EARLY]):
        share(EARLY, c)
    for copy in loads:
        copy.start()
    arrive(meta_early)
    meta_x = meta_link(0, 2, at_x)
    meta_y = meta_link(0, 4, at_y)
    meta_core = meta_link(0, 1, at_core)
    arrive(meta_x)
    meta_d = meta_link(2, 6, at_y)
    meta_core += meta_link(2, 3, at_core)
    arrive(meta_y)
    meta_core += meta_link(4, 5, at_core)
    for copy in loads:
        copy.wait()
    arrive(meta_core[:2])
    expert(EARLY, OWN)
    for c in range(chunks[EARLY]):
        relay(EARLY, c)
    arrive(meta_d)
    meta_core += meta_link(6, 7, at_core)
    for c in range(chunks[LATE]):
        hop[c].wait_recv()
        share(LATE, c)
    arrive(meta_core[2:])
    expert(EARLY, ACROSS_X)
    for c in range(chunks[EARLY]):
        relay_diagonal(EARLY, c)
    expert(EARLY, ACROSS_Y)
    expert(EARLY, DIAGONAL)
    for c in range(chunks[LATE]):
        relay(LATE, c)
    send_diagonal(EARLY)
    send_direct(EARLY)
    expert(LATE, OWN)
    expert(LATE, ACROSS_X)
    for c in range(chunks[LATE]):
        relay_diagonal(LATE, c)
    expert(LATE, ACROSS_Y)
    send_merged(EARLY)
    expert(LATE, DIAGONAL)
    send_diagonal(LATE)
    send_direct(LATE)
    finish(EARLY)
    send_merged(LATE)
    finish(LATE)
    arrive(home)
    for copy in started:
        copy.wait_send()


def fused(incoming, expert_ids, gate_scores, gate_proj, up_proj, down_proj):
    _, rows, features = incoming.shape
    top, ff = expert_ids.shape[2], gate_proj.shape[2]
    n_pp, n_tp, n_ep = (lax.axis_size(a) for a in ("pp", "tp", "ep"))
    early = rows // 2
    groups = (early, rows - early)
    chunks, pieces = (4, 4), 2
    hbm, vmem = pl.BlockSpec(memory_space=pl.ANY), pl.BlockSpec(memory_space=pltpu.VMEM)
    narrow = functools.partial(pltpu.VMEM, dtype=jnp.bfloat16)
    copies = 8 * sum(chunks) + 2 * 8 + 2 * 4 + 8 * 2 * pieces

    def pair(*lead):
        return [narrow((*lead, n, features)) for n in groups]

    return pl.pallas_call(
        functools.partial(exchange_kernel, (n_pp, n_tp, n_ep, top, chunks, pieces)),
        out_shape=pltpu.VMEM(incoming.shape, incoming.dtype),
        in_specs=[hbm] * 6,
        out_specs=vmem,
        scratch_shapes=[
            narrow((features, ff)),
            narrow((features, ff)),
            narrow((ff, features)),
            *pair(4, 2),
            pltpu.VMEM((8, 2, top, rows), jnp.int32),
            pltpu.VMEM((8, 2, top, rows), jnp.float32),
            narrow((2 * max(groups), ff)),
            *pair(4),
            *pair(4),
            *pair(4),
            *pair(3),
            *pair(2),
            *pair(1),
            narrow((early, features)),
            pltpu.SemaphoreType.DMA((copies,)),
            pltpu.SemaphoreType.DMA((copies,)),
            pltpu.SemaphoreType.DMA((6,)),
        ],
        compiler_params=pltpu.CompilerParams(collective_id=0, has_side_effects=True),
    )(incoming, expert_ids[0].T, gate_scores[0].T, gate_proj, up_proj, down_proj)


def solution(mesh):
    placed = (
        P("pp", ("tp", "ep"), None),
        P("pp", ("tp", "ep"), None),
        P("pp", ("tp", "ep"), None),
        P(("tp", "ep"), None, None),
        P(("tp", "ep"), None, None),
        P(("tp", "ep"), None, None),
    )
    square = mesh.shape["tp"] == 4 and mesh.shape["ep"] == 2 and mesh.shape["pp"] > 1
    return jax.shard_map(
        fused if square else shards,
        mesh=mesh,
        in_specs=placed,
        out_specs=P("pp", ("tp", "ep"), None),
        check_vma=False,
    )
```

time: 51 us -> 49.5 us (0.971)
  Pallas kernels: 50.1 us -> 48.5 us
    pallas_call x1, Pallas kernels: 50.1 us -> 48.5 us  [fused(): pl.pallas_call(functools.partial(exchange_kernel, (n_pp, n_tp, n_ep, top,...]
where the time goes in v1:
time: 49.5 us; the launch traced here: 49.4 us
  Pallas kernels  48.5 us (98%)
  local copies, waits for them, and re-layouts  0.8 us (2%)
    pallas_call x1, Pallas kernels, fused(): pl.pallas_call(functools.partial(exchange_kernel, (n_pp, n_tp, n_ep, top,...  48.5 us

profile of v1, /device:TPU:0, one launch (start us, length us, event | category | flops | bytes accessed | tf_op | source)
XLA Modules:
  0.0 49.4 jit_solution(4893781039620225586)
XLA Ops:
  0.0 48.5 %shard_map.64 = bf16[1,128,2048]{2,1,0:T(8,128)(2,1)S(1)} custom-call(bf16[1,128,2048]{2,1,0:T(8,128)(2,1)} %incoming.1, s32[2,128]{1,0:T(2,128)} %bitcast.6, f32[2,128]{1,0:T(2,128)} %bitcast.7, bf16[1,2048,768]{2,1,0:T(8,128)(2,1)} %gate_hbm.1, bf16[1,2048,768]{2,1,0:T(8,128)(2,1)} %up_hbm.1, bf16[1,768,2048]{2,1,0:T(8,128)(2,1)} %down_hbm.1), custom_call_target="tpu_custom_call" | custom-call | tf_op jit(solution)/shard_map/pallas_call | solution.py:368
  48.6 0.8 %copy.8 = bf16[1,128,2048]{2,1,0:T(8,128)(2,1)} copy(bf16[1,128,2048]{2,1,0:T(8,128)(2,1)S(1)} %shard_map.64) | data formatting | bytes 1048576

commit v2 on v1

v2 whole, which is shorter than its diff:
```python
import functools

import jax
import jax.numpy as jnp
from jax import lax
from jax.experimental import pallas as pl
from jax.experimental.pallas import tpu as pltpu
from jax.sharding import PartitionSpec as P

MESH = pl.DeviceIdType.MESH
OWN, ACROSS_X, ACROSS_Y, DIAGONAL = range(4)
EARLY, LATE = range(2)


def shifted(block, axis, distance):
    devices = range(lax.axis_size(axis))
    route = [((i - distance) % len(devices), i) for i in devices]
    return lax.ppermute(block, axis, route)


def expert_apply(tokens_in, gate_mat, up_mat, down_mat):
    gate_part = jnp.dot(tokens_in, gate_mat, preferred_element_type=jnp.float32)
    upward = jnp.dot(tokens_in, up_mat, preferred_element_type=jnp.float32)
    hidden = (jax.nn.silu(gate_part) * upward).astype(jnp.bfloat16)
    return jnp.dot(hidden, down_mat, preferred_element_type=jnp.float32).astype(jnp.bfloat16)


def shards(incoming, expert_ids, gate_scores, gate_proj, up_proj, down_proj):
    arrived = shifted(incoming, "pp", 1)[0]
    tok_count, features = arrived.shape
    top_count = expert_ids.shape[2]
    expert_count = lax.axis_size("tp") * lax.axis_size("ep")
    capacity = min(tok_count, 2 * tok_count * top_count // expert_count)
    values = arrived.astype(jnp.float32)
    normed = (values * lax.rsqrt(jnp.mean(values * values, axis=1, keepdims=True) + 1e-06)).astype(
        jnp.bfloat16
    )
    chosen = expert_ids[0].reshape(-1)
    onehot = (chosen[:, None] == jnp.arange(expert_count, dtype=jnp.int32)[None, :]).astype(
        jnp.int32
    )
    before = jnp.cumsum(onehot, axis=0) - onehot
    slot_of = jnp.sum(before * onehot, axis=1)
    destination = chosen * capacity + slot_of
    owner_row = jnp.arange(chosen.shape[0], dtype=jnp.int32) // top_count
    source_row = (
        jnp.full((expert_count * capacity,), tok_count, jnp.int32).at[destination].set(owner_row)
    )
    occupied = jnp.zeros((expert_count * capacity,), jnp.int32).at[destination].set(1)
    with_blank = jnp.concatenate([normed, jnp.zeros((1, features), jnp.bfloat16)], axis=0)
    outgoing = with_blank[source_row].reshape(expert_count, capacity, features)
    occupied = occupied.reshape(expert_count, capacity)
    gate_mat, up_mat, down_mat = (gate_proj[0], up_proj[0], down_proj[0])
    received_rows = lax.all_to_all(outgoing, ("tp", "ep"), split_axis=0, concat_axis=0, tiled=True)
    flat_rows = received_rows.reshape(-1, features)
    flat_live = lax.all_to_all(
        occupied, ("tp", "ep"), split_axis=0, concat_axis=0, tiled=True
    ).reshape(-1)
    answered = expert_apply(flat_rows, gate_mat, up_mat, down_mat) * flat_live[:, None].astype(
        jnp.bfloat16
    )
    answered = answered.reshape(received_rows.shape)
    returned = lax.all_to_all(answered, ("tp", "ep"), split_axis=0, concat_axis=0, tiled=True)
    picked = returned.reshape(expert_count * capacity, features)[destination].reshape(
        tok_count, top_count, features
    )
    scores = gate_scores[0]
    weights = scores / jnp.sum(scores, axis=1, keepdims=True)
    combined = values + jnp.sum(weights[:, :, None] * picked.astype(jnp.float32), axis=1)
    return combined.astype(jnp.bfloat16)[None]


def exchange_kernel(
    sizes,
    incoming,
    ids_hbm,
    scores_hbm,
    gate_hbm,
    up_hbm,
    down_hbm,
    out_ref,
    gate_w,
    up_w,
    down_w,
    tok_early,
    tok_late,
    own_ids,
    own_scores,
    meta,
    hidden,
    kept_early,
    kept_late,
    passed_early,
    passed_late,
    partner_early,
    partner_late,
    to_early,
    to_late,
    from_early,
    from_late,
    via_early,
    via_late,
    done_early,
    send_sem,
    recv_sem,
    load_sem,
):
    n_pp, n_tp, n_ep, top, chunks, pieces = sizes
    features, ff = gate_w.shape
    pp, tp, ep = lax.axis_index("pp"), lax.axis_index("tp"), lax.axis_index("ep")
    other_core = tp + 1 - 2 * (tp % 2)
    at_x = {"ep": (ep + 1) % n_ep}
    at_y = {"tp": (tp + 2) % n_tp}
    at_core = {"tp": other_core}
    across = {"ep": (ep + 1) % n_ep, "tp": (tp + 2) % n_tp}
    ahead, behind = {"pp": (pp + 1) % n_pp}, {"pp": (pp + n_pp - 1) % n_pp}

    tok = (tok_early, tok_late)
    kept, passed = (kept_early, kept_late), (passed_early, passed_late)
    partner = (partner_early, partner_late)
    to, landed, via = (to_early, to_late), (from_early, from_late), (via_early, via_late)
    count = [t.shape[1] for t in tok]
    first_row = [count[LATE], 0]
    half = [n // 2 for n in count]
    part = [[pl.ds(c * (n // m), n // m) for c in range(m)] for n, m in zip(count, chunks)]

    loads = []
    for src, dst in ((gate_hbm, gate_w), (up_hbm, up_w), (down_hbm, down_w)):
        loads.append(pltpu.make_async_copy(src.at[0], dst, load_sem.at[len(loads)]))
    own_rows = pltpu.make_async_copy(
        incoming.at[0, pl.ds(first_row[EARLY], count[EARLY])], tok_early.at[0], load_sem.at[3]
    )
    own_meta = [
        pltpu.make_async_copy(ids_hbm, own_ids, load_sem.at[4]),
        pltpu.make_async_copy(scores_hbm, own_scores, load_sem.at[5]),
    ]

    barrier = pltpu.get_barrier_semaphore()
    for peer in (at_x, at_y, at_core, ahead, behind):
        pl.semaphore_signal(barrier, inc=1, device_id=peer, device_id_type=MESH)
    for copy in own_meta:
        copy.start()
    own_rows.start()
    for copy in own_meta:
        copy.wait()

    def meta_slot(g, source):
        return 8 * g + source

    scores = own_scores[...]
    meta[meta_slot(LATE, 0), :top] = own_ids[...].astype(jnp.float32)
    meta[meta_slot(LATE, 0), top:] = scores / jnp.sum(scores, axis=0, keepdims=True)
    own_rows.wait()
    pl.semaphore_wait(barrier, 5)

    lanes, sends = {}, {}

    def link(src, dst, peer, arrives, leaves):
        copy = pltpu.make_async_remote_copy(
            src_ref=src,
            dst_ref=dst,
            send_sem=send_sem.at[sends.setdefault(leaves, len(sends))],
            recv_sem=recv_sem.at[lanes.setdefault(arrives, len(lanes))],
            device_id=peer,
            device_id_type=MESH,
        )
        copy.start()

    def arrive(key, ref):
        sem = recv_sem.at[lanes[key]]
        pltpu.make_async_copy(ref, ref, sem).wait()

    def left(key, ref):
        sem = send_sem.at[sends[key]]
        pltpu.make_async_copy(ref, ref, sem).wait()

    def block(g, role, side, c):
        return tok[g].at[2 * role + side, part[g][c]]

    def share(g, c):
        link(block(g, OWN, 0, c), block(g, ACROSS_X, 0, c), at_x, (g, "x", c), (g, "gather"))
        link(block(g, OWN, 0, c), block(g, ACROSS_Y, 0, c), at_y, (g, "y", c), (g, "gather"))
        to_core(g, OWN, c)

    def to_core(g, role, c):
        link(block(g, role, 0, c), block(g, role, 1, c), at_core, (g, "core", role), (g, "gather"))

    def relay(g, c):
        arrive((g, "x", c), block(g, ACROSS_X, 0, c))
        if c % 2 == 0:
            link(
                block(g, ACROSS_X, 0, c), block(g, DIAGONAL, 0, c), at_y, (g, "d", c), (g, "gather")
            )
        to_core(g, ACROSS_X, c)
        arrive((g, "y", c), block(g, ACROSS_Y, 0, c))
        if c % 2 == 1:
            link(
                block(g, ACROSS_Y, 0, c), block(g, DIAGONAL, 0, c), at_x, (g, "d", c), (g, "gather")
            )
        to_core(g, ACROSS_Y, c)

    def relay_diagonal(g, c):
        arrive((g, "d", c), block(g, DIAGONAL, 0, c))
        to_core(g, DIAGONAL, c)

    def meta_link(g, src, dst, peer, name):
        src, dst = meta_slot(g, src), meta_slot(g, dst)
        link(meta.at[src], meta.at[dst], peer, (g, "meta", name), "meta")

    def meta_arrive(g, name, n=1):
        arrive((g, "meta", name), meta.at[pl.ds(0, n)])

    def meta_first(g):
        meta_link(g, 0, 2, at_x, "x")
        meta_link(g, 0, 4, at_y, "y")
        meta_link(g, 0, 1, at_core, "near")

    def meta_second(g):
        if g == LATE:
            meta_link(g, 2, 6, at_y, "d")
        else:
            meta_arrive(g, "x")
            meta_arrive(g, "y")
        meta_link(g, 2, 3, at_core, "near")
        meta_link(g, 4, 5, at_core, "near")

    def meta_third(g):
        meta_arrive(g, "d")
        meta_link(g, 6, 7, at_core, "far")

    mine = (tp * n_ep + ep).astype(jnp.float32)

    def weight(g, role):
        columns = []
        lane = lax.broadcasted_iota(jnp.int32, (count[g], meta.shape[2]), 1)
        row = lax.broadcasted_iota(jnp.int32, (count[g], meta.shape[2]), 0)
        for side in range(2):
            source = meta[meta_slot(g, 2 * role + side)]
            named = jnp.where(source[:top] == mine, source[top:], 0.0)
            named = jnp.sum(named, axis=0, keepdims=True)
            columns.append(
                jnp.sum(jnp.where(lane == row + first_row[g], named, 0.0), axis=1, keepdims=True)
            )
        return columns

    def expert(g, role):
        arrive((g, "core", role), tok[g].at[2 * role + 1])
        n = count[g]
        tokens_in = tok[g][2 * role : 2 * role + 2].reshape(2 * n, features)
        values = tokens_in.astype(jnp.float32)
        scale = lax.rsqrt(jnp.mean(values * values, axis=1, keepdims=True) + 1e-06)
        step = 256 if ff % 256 == 0 else 128
        for j in range(ff // step):
            cols = pl.ds(j * step, step)
            gate = jnp.dot(tokens_in, gate_w[:, cols], preferred_element_type=jnp.float32) * scale
            upward = jnp.dot(tokens_in, up_w[:, cols], preferred_element_type=jnp.float32) * scale
            hidden[: 2 * n, cols] = (gate / (1.0 + jnp.exp(-gate)) * upward).astype(jnp.bfloat16)
        inner = hidden[: 2 * n]
        here, there = weight(g, role)
        for j in range(features // 256):
            cols = pl.ds(j * 256, 256)
            y = jnp.dot(inner, down_w[:, cols], preferred_element_type=jnp.float32)
            y = y.astype(jnp.bfloat16).astype(jnp.float32)
            kept[g][role, :, cols] = (y[:n] * here).astype(jnp.bfloat16)
            passed[g][role, :, cols] = (y[n:] * there).astype(jnp.bfloat16)
        link(passed[g].at[role], partner[g].at[role], at_core, (g, "swap", role), (g, "return"))

    def swapped(g, role):
        arrive((g, "swap", role), partner[g].at[role])

    def summed(g, role, lo, hi):
        return kept[g][role, lo:hi].astype(jnp.float32) + partner[g][role, lo:hi].astype(jnp.float32)

    def cuts(g):
        size = half[g] // pieces
        return [(p * size, (p + 1) * size) for p in range(pieces)]

    def post(g, buffer, landing, lo, hi, value, peer, arrives):
        to[g][buffer, lo:hi] = value.astype(jnp.bfloat16)
        rows = pl.ds(lo, hi - lo)
        link(to[g].at[buffer, rows], landing.at[rows], peer, (g, *arrives), (g, "return"))

    def send_diagonal(g):
        swapped(g, DIAGONAL)
        for p, (lo, hi) in enumerate(cuts(g)):
            value = summed(g, DIAGONAL, lo, hi)
            post(g, 2, via[g], lo, hi, value, at_x, ("across", 0, p))
            lo, hi = lo + half[g], hi + half[g]
            value = summed(g, DIAGONAL, lo, hi)
            post(g, 2, via[g], lo, hi, value, at_y, ("across", 1, p))

    def send_direct(g):
        swapped(g, ACROSS_X)
        swapped(g, ACROSS_Y)
        for lo, hi in cuts(g):
            value = summed(g, ACROSS_X, lo, hi)
            post(g, 0, landed[g].at[0], lo, hi, value, at_x, ("direct", 0))
            lo, hi = lo + half[g], hi + half[g]
            value = summed(g, ACROSS_Y, lo, hi)
            post(g, 1, landed[g].at[1], lo, hi, value, at_y, ("direct", 1))

    def send_merged(g):
        for p, (lo, hi) in enumerate(cuts(g)):
            arrive((g, "across", 0, p), via[g].at[pl.ds(lo, hi - lo)])
            value = summed(g, ACROSS_Y, lo, hi) + via[g][lo:hi].astype(jnp.float32)
            post(g, 1, landed[g].at[1], lo, hi, value, at_y, ("merged", 0, p))
            lo, hi = lo + half[g], hi + half[g]
            arrive((g, "across", 1, p), via[g].at[pl.ds(lo, hi - lo)])
            value = summed(g, ACROSS_X, lo, hi) + via[g][lo:hi].astype(jnp.float32)
            post(g, 0, landed[g].at[0], lo, hi, value, at_x, ("merged", 1, p))

    def finish(g):
        swapped(g, OWN)
        for k in range(2):
            arrive((g, "direct", k), via[g].at[pl.ds(0, half[g])])
        for p, span in enumerate(cuts(g)):
            for k in range(2):
                lo, hi = (edge + k * half[g] for edge in span)
                value = summed(g, OWN, lo, hi) + tok[g][0, lo:hi].astype(jnp.float32)
                value += landed[g][k, lo:hi].astype(jnp.float32)
                arrive((g, "merged", k, p), landed[g].at[1 - k, pl.ds(lo, hi - lo)])
                value += landed[g][1 - k, lo:hi].astype(jnp.float32)
                value = value.astype(jnp.bfloat16)
                if g == LATE:
                    out_ref[0, lo:hi] = value
                else:
                    done_early[lo:hi] = value
                    cut = pl.ds(lo + first_row[g], hi - lo)
                    link(done_early.at[pl.ds(lo, hi - lo)], out_ref.at[0, cut], ahead, "home", "home")

    meta_link_back = (meta.at[meta_slot(LATE, 0)], meta.at[meta_slot(EARLY, 0)])
    link(*meta_link_back, behind, (EARLY, "meta", "own"), "meta")
    meta_first(LATE)
    for c in range(chunks[LATE]):
        link(incoming.at[0, part[LATE][c]], block(LATE, OWN, 0, c), ahead, ("hop", c), "hop")
    for c in range(chunks[EARLY] - 1):
        share(EARLY, c)
    for copy in loads:
        copy.start()
    meta_arrive(LATE, "x")
    meta_arrive(EARLY, "own")
    meta_first(EARLY)
    meta_link(EARLY, 0, 6, across, "d")
    share(EARLY, chunks[EARLY] - 1)
    meta_arrive(LATE, "y")
    meta_second(LATE)
    lag = chunks[EARLY] // 2
    for c in range(max(chunks[EARLY], chunks[LATE] + lag)):
        if c < chunks[EARLY]:
            relay(EARLY, c)
        if 0 <= c - lag < chunks[LATE]:
            arrive(("hop", c - lag), block(LATE, OWN, 0, c - lag))
            share(LATE, c - lag)
    meta_second(EARLY)
    meta_third(LATE)
    for copy in loads:
        copy.wait()
    meta_arrive(EARLY, "near", 3)
    expert(EARLY, ACROSS_X)
    meta_third(EARLY)
    expert(EARLY, ACROSS_Y)
    for c in range(chunks[EARLY]):
        relay_diagonal(EARLY, c)
    relay(LATE, 0)
    meta_arrive(EARLY, "far")
    expert(EARLY, DIAGONAL)
    for c in range(1, chunks[LATE]):
        relay(LATE, c)
    send_diagonal(EARLY)
    send_direct(EARLY)
    expert(EARLY, OWN)
    meta_arrive(LATE, "near", 3)
    meta_arrive(LATE, "far")
    expert(LATE, ACROSS_X)
    for c in range(chunks[LATE]):
        relay_diagonal(LATE, c)
    expert(LATE, ACROSS_Y)
    expert(LATE, DIAGONAL)
    send_merged(EARLY)
    send_diagonal(LATE)
    send_direct(LATE)
    expert(LATE, OWN)
    finish(EARLY)
    send_merged(LATE)
    finish(LATE)
    arrive("home", tok_early.at[0])
    left("hop", tok_late.at[0])
    left("home", tok_early.at[0])
    for g in (EARLY, LATE):
        left((g, "gather"), tok[g].at[pl.ds(0, 7)])
        left((g, "return"), tok[g].at[pl.ds(0, 7)])
    left("meta", meta.at[pl.ds(0, 15)])


def fused(incoming, expert_ids, gate_scores, gate_proj, up_proj, down_proj):
    _, rows, features = incoming.shape
    top, ff = expert_ids.shape[2], gate_proj.shape[2]
    n_pp, n_tp, n_ep = (lax.axis_size(a) for a in ("pp", "tp", "ep"))
    early = rows // 2
    groups = (early, rows - early)
    chunks, pieces = (4, 4), 2
    hbm, vmem = pl.BlockSpec(memory_space=pl.ANY), pl.BlockSpec(memory_space=pltpu.VMEM)
    narrow = functools.partial(pltpu.VMEM, dtype=jnp.bfloat16)
    arrivals = 3 * sum(chunks) + 8 + 8 + 2 * (4 * pieces + 2) + 1 + chunks[1] + 11

    def pair(*lead):
        return [narrow((*lead, n, features)) for n in groups]

    return pl.pallas_call(
        functools.partial(exchange_kernel, (n_pp, n_tp, n_ep, top, chunks, pieces)),
        out_shape=pltpu.VMEM(incoming.shape, incoming.dtype),
        in_specs=[hbm] * 6,
        out_specs=vmem,
        scratch_shapes=[
            narrow((features, ff)),
            narrow((features, ff)),
            narrow((ff, features)),
            *pair(8),
            pltpu.VMEM((top, rows), jnp.int32),
            pltpu.VMEM((top, rows), jnp.float32),
            pltpu.VMEM((16, 2 * top, rows), jnp.float32),
            narrow((2 * max(groups), ff)),
            *pair(4),
            *pair(4),
            *pair(4),
            *pair(3),
            *pair(2),
            *pair(),
            narrow((early, features)),
            pltpu.SemaphoreType.DMA((7,)),
            pltpu.SemaphoreType.DMA((arrivals,)),
            pltpu.SemaphoreType.DMA((6,)),
        ],
        compiler_params=pltpu.CompilerParams(collective_id=0, has_side_effects=True),
    )(incoming, expert_ids[0].T, gate_scores[0].T, gate_proj, up_proj, down_proj)


def solution(mesh):
    placed = (
        P("pp", ("tp", "ep"), None),
        P("pp", ("tp", "ep"), None),
        P("pp", ("tp", "ep"), None),
        P(("tp", "ep"), None, None),
        P(("tp", "ep"), None, None),
        P(("tp", "ep"), None, None),
    )
    square = mesh.shape["tp"] == 4 and mesh.shape["ep"] == 2 and mesh.shape["pp"] > 1
    return jax.shard_map(
        fused if square else shards,
        mesh=mesh,
        in_specs=placed,
        out_specs=P("pp", ("tp", "ep"), None),
        check_vma=False,
    )
```

time: 49.5 us -> 44.5 us (0.90)
  Pallas kernels: 48.5 us -> 43.6 us
    pallas_call x1, Pallas kernels: 48.5 us -> 43.6 us  [fused(): pl.pallas_call(functools.partial(exchange_kernel, (n_pp, n_tp, n_ep, top,...]
where the time goes in v2:
time: 44.5 us; the launch traced here: 44.4 us
  Pallas kernels  43.6 us (98%)
  local copies, waits for them, and re-layouts  0.8 us (2%)
    pallas_call x1, Pallas kernels, fused(): pl.pallas_call(functools.partial(exchange_kernel, (n_pp, n_tp, n_ep, top,...  43.6 us

profile of v2, /device:TPU:0, one launch (start us, length us, event | category | flops | bytes accessed | tf_op | source)
XLA Modules:
  0.0 44.4 jit_solution(2290159621501907510)
XLA Ops:
  0.0 43.6 %shard_map.64 = bf16[1,128,2048]{2,1,0:T(8,128)(2,1)S(1)} custom-call(bf16[1,128,2048]{2,1,0:T(8,128)(2,1)} %incoming.1, s32[2,128]{1,0:T(2,128)} %bitcast.6, f32[2,128]{1,0:T(2,128)} %bitcast.7, bf16[1,2048,768]{2,1,0:T(8,128)(2,1)} %gate_hbm.1, bf16[1,2048,768]{2,1,0:T(8,128)(2,1)} %up_hbm.1, bf16[1,768,2048]{2,1,0:T(8,128)(2,1)} %down_hbm.1), custom_call_target="tpu_custom_call" | custom-call | tf_op jit(solution)/shard_map/pallas_call | solution.py:409
  43.6 0.8 %copy.8 = bf16[1,128,2048]{2,1,0:T(8,128)(2,1)} copy(bf16[1,128,2048]{2,1,0:T(8,128)(2,1)S(1)} %shard_map.64) | data formatting | bytes 1048576

commit v3 on v2

--- a/solution.py
+++ b/solution.py
@@ -104,6 +104,7 @@
     send_sem,
     recv_sem,
     load_sem,
+    hello,
 ):
     n_pp, n_tp, n_ep, top, chunks, pieces = sizes
     features, ff = gate_w.shape
@@ -136,7 +137,7 @@
     ]
 
     barrier = pltpu.get_barrier_semaphore()
-    for peer in (at_x, at_y, at_core, ahead, behind):
+    for peer in (at_x, at_y, at_core, behind):
         pl.semaphore_signal(barrier, inc=1, device_id=peer, device_id_type=MESH)
     for copy in own_meta:
         copy.start()
@@ -151,7 +152,8 @@
     meta[meta_slot(LATE, 0), :top] = own_ids[...].astype(jnp.float32)
     meta[meta_slot(LATE, 0), top:] = scores / jnp.sum(scores, axis=0, keepdims=True)
     own_rows.wait()
-    pl.semaphore_wait(barrier, 5)
+    pl.semaphore_wait(barrier, 4)
+    pl.semaphore_signal(hello, inc=1, device_id=ahead, device_id_type=MESH)
 
     lanes, sends = {}, {}
 
@@ -243,7 +245,7 @@
             )
         return columns
 
-    def expert(g, role):
+    def expert(g, role, between=lambda: None):
         arrive((g, "core", role), tok[g].at[2 * role + 1])
         n = count[g]
         tokens_in = tok[g][2 * role : 2 * role + 2].reshape(2 * n, features)
@@ -256,6 +258,7 @@
             upward = jnp.dot(tokens_in, up_w[:, cols], preferred_element_type=jnp.float32) * scale
             hidden[: 2 * n, cols] = (gate / (1.0 + jnp.exp(-gate)) * upward).astype(jnp.bfloat16)
         inner = hidden[: 2 * n]
+        between()
         here, there = weight(g, role)
         for j in range(features // 256):
             cols = pl.ds(j * 256, 256)
@@ -294,31 +297,30 @@
         swapped(g, ACROSS_Y)
         for lo, hi in cuts(g):
             value = summed(g, ACROSS_X, lo, hi)
-            post(g, 0, landed[g].at[0], lo, hi, value, at_x, ("direct", 0))
+            post(g, 0, landed[g].at[0], lo, hi, value, at_x, ("direct",))
             lo, hi = lo + half[g], hi + half[g]
             value = summed(g, ACROSS_Y, lo, hi)
-            post(g, 1, landed[g].at[1], lo, hi, value, at_y, ("direct", 1))
+            post(g, 1, landed[g].at[1], lo, hi, value, at_y, ("direct",))
 
     def send_merged(g):
         for p, (lo, hi) in enumerate(cuts(g)):
             arrive((g, "across", 0, p), via[g].at[pl.ds(lo, hi - lo)])
             value = summed(g, ACROSS_Y, lo, hi) + via[g][lo:hi].astype(jnp.float32)
-            post(g, 1, landed[g].at[1], lo, hi, value, at_y, ("merged", 0, p))
+            post(g, 1, landed[g].at[1], lo, hi, value, at_y, ("merged", p))
             lo, hi = lo + half[g], hi + half[g]
             arrive((g, "across", 1, p), via[g].at[pl.ds(lo, hi - lo)])
             value = summed(g, ACROSS_X, lo, hi) + via[g][lo:hi].astype(jnp.float32)
-            post(g, 0, landed[g].at[0], lo, hi, value, at_x, ("merged", 1, p))
+            post(g, 0, landed[g].at[0], lo, hi, value, at_x, ("merged", p))
 
     def finish(g):
         swapped(g, OWN)
-        for k in range(2):
-            arrive((g, "direct", k), via[g].at[pl.ds(0, half[g])])
+        arrive((g, "direct"), via[g])
         for p, span in enumerate(cuts(g)):
+            arrive((g, "merged", p), via[g].at[pl.ds(0, 2 * (span[1] - span[0]))])
             for k in range(2):
                 lo, hi = (edge + k * half[g] for edge in span)
                 value = summed(g, OWN, lo, hi) + tok[g][0, lo:hi].astype(jnp.float32)
                 value += landed[g][k, lo:hi].astype(jnp.float32)
-                arrive((g, "merged", k, p), landed[g].at[1 - k, pl.ds(lo, hi - lo)])
                 value += landed[g][1 - k, lo:hi].astype(jnp.float32)
                 value = value.astype(jnp.bfloat16)
                 if g == LATE:
@@ -328,8 +330,10 @@
                     cut = pl.ds(lo + first_row[g], hi - lo)
                     link(done_early.at[pl.ds(lo, hi - lo)], out_ref.at[0, cut], ahead, "home", "home")
 
-    meta_link_back = (meta.at[meta_slot(LATE, 0)], meta.at[meta_slot(EARLY, 0)])
-    link(*meta_link_back, behind, (EARLY, "meta", "own"), "meta")
+    def near():
+        meta_second(EARLY)
+        meta_arrive(EARLY, "near", 3)
+
     meta_first(LATE)
     for c in range(chunks[LATE]):
         link(incoming.at[0, part[LATE][c]], block(LATE, OWN, 0, c), ahead, ("hop", c), "hop")
@@ -337,26 +341,28 @@
         share(EARLY, c)
     for copy in loads:
         copy.start()
+    pl.semaphore_wait(hello, 1)
+    meta_link_back = (meta.at[meta_slot(LATE, 0)], meta.at[meta_slot(EARLY, 0)])
+    link(*meta_link_back, behind, (EARLY, "meta", "own"), "meta")
+    share(EARLY, chunks[EARLY] - 1)
     meta_arrive(LATE, "x")
-    meta_arrive(EARLY, "own")
-    meta_first(EARLY)
-    meta_link(EARLY, 0, 6, across, "d")
-    share(EARLY, chunks[EARLY] - 1)
     meta_arrive(LATE, "y")
     meta_second(LATE)
     lag = chunks[EARLY] // 2
     for c in range(max(chunks[EARLY], chunks[LATE] + lag)):
+        if c == lag:
+            meta_arrive(EARLY, "own")
+            meta_first(EARLY)
+            meta_link(EARLY, 0, 6, across, "d")
         if c < chunks[EARLY]:
             relay(EARLY, c)
         if 0 <= c - lag < chunks[LATE]:
             arrive(("hop", c - lag), block(LATE, OWN, 0, c - lag))
             share(LATE, c - lag)
-    meta_second(EARLY)
     meta_third(LATE)
     for copy in loads:
         copy.wait()
-    meta_arrive(EARLY, "near", 3)
-    expert(EARLY, ACROSS_X)
+    expert(EARLY, ACROSS_X, near)
     meta_third(EARLY)
     expert(EARLY, ACROSS_Y)
     for c in range(chunks[EARLY]):
@@ -401,7 +407,7 @@
     chunks, pieces = (4, 4), 2
     hbm, vmem = pl.BlockSpec(memory_space=pl.ANY), pl.BlockSpec(memory_space=pltpu.VMEM)
     narrow = functools.partial(pltpu.VMEM, dtype=jnp.bfloat16)
-    arrivals = 3 * sum(chunks) + 8 + 8 + 2 * (4 * pieces + 2) + 1 + chunks[1] + 11
+    arrivals = 3 * sum(chunks) + 8 + 8 + 2 * (3 * pieces + 1) + 1 + chunks[1] + 11
 
     def pair(*lead):
         return [narrow((*lead, n, features)) for n in groups]
@@ -430,6 +436,7 @@
             pltpu.SemaphoreType.DMA((7,)),
             pltpu.SemaphoreType.DMA((arrivals,)),
             pltpu.SemaphoreType.DMA((6,)),
+            pltpu.SemaphoreType.REGULAR,
         ],
         compiler_params=pltpu.CompilerParams(collective_id=0, has_side_effects=True),
     )(incoming, expert_ids[0].T, gate_scores[0].T, gate_proj, up_proj, down_proj)

time: 44.5 us -> 43.2 us (0.971)
  Pallas kernels: 43.6 us -> 42.2 us
    pallas_call x1, Pallas kernels: 43.6 us -> 42.2 us  [fused(): pl.pallas_call(functools.partial(exchange_kernel, (n_pp, n_tp, n_ep, top,...]
where the time goes in v3:
time: 43.2 us; the launch traced here: 43 us
  Pallas kernels  42.2 us (98%)
  local copies, waits for them, and re-layouts  0.8 us (2%)
    pallas_call x1, Pallas kernels, fused(): pl.pallas_call(functools.partial(exchange_kernel, (n_pp, n_tp, n_ep, top,...  42.2 us

profile of v3, /device:TPU:0, one launch (start us, length us, event | category | flops | bytes accessed | tf_op | source)
XLA Modules:
  0.0 43.0 jit_solution(11545121894897702813)
XLA Ops:
  0.0 42.2 %shard_map.64 = bf16[1,128,2048]{2,1,0:T(8,128)(2,1)S(1)} custom-call(bf16[1,128,2048]{2,1,0:T(8,128)(2,1)} %incoming.1, s32[2,128]{1,0:T(2,128)} %bitcast.6, f32[2,128]{1,0:T(2,128)} %bitcast.7, bf16[1,2048,768]{2,1,0:T(8,128)(2,1)} %gate_hbm.1, bf16[1,2048,768]{2,1,0:T(8,128)(2,1)} %up_hbm.1, bf16[1,768,2048]{2,1,0:T(8,128)(2,1)} %down_hbm.1), custom_call_target="tpu_custom_call" | custom-call | tf_op jit(solution)/shard_map/pallas_call | solution.py:415
  42.3 0.8 %copy.8 = bf16[1,128,2048]{2,1,0:T(8,128)(2,1)} copy(bf16[1,128,2048]{2,1,0:T(8,128)(2,1)S(1)} %shard_map.64) | data formatting | bytes 1048576

commit v4 on v3

--- a/solution.py
+++ b/solution.py
@@ -123,7 +123,7 @@
     count = [t.shape[1] for t in tok]
     first_row = [count[LATE], 0]
     half = [n // 2 for n in count]
-    part = [[pl.ds(c * (n // m), n // m) for c in range(m)] for n, m in zip(count, chunks)]
+    part = [[pl.ds(c * (n // chunks), n // chunks) for c in range(chunks)] for n in count]
 
     loads = []
     for src, dst in ((gate_hbm, gate_w), (up_hbm, up_w), (down_hbm, down_w)):
@@ -179,27 +179,28 @@
     def block(g, role, side, c):
         return tok[g].at[2 * role + side, part[g][c]]
 
+    def share_x(g, c):
+        link(block(g, OWN, 0, c), block(g, ACROSS_X, 0, c), at_x, (g, "x", c), (g, "gather"))
+        to_core(g, OWN, c)
+
+    def share_y(g, c):
+        link(block(g, OWN, 0, c), block(g, ACROSS_Y, 0, c), at_y, (g, "y", c), (g, "gather"))
+
     def share(g, c):
-        link(block(g, OWN, 0, c), block(g, ACROSS_X, 0, c), at_x, (g, "x", c), (g, "gather"))
-        link(block(g, OWN, 0, c), block(g, ACROSS_Y, 0, c), at_y, (g, "y", c), (g, "gather"))
-        to_core(g, OWN, c)
+        share_x(g, c)
+        if c % 2 == 1:
+            share_y(g, c)
+            share_y(g, c - 1)
 
     def to_core(g, role, c):
         link(block(g, role, 0, c), block(g, role, 1, c), at_core, (g, "core", role), (g, "gather"))
 
     def relay(g, c):
-        arrive((g, "x", c), block(g, ACROSS_X, 0, c))
-        if c % 2 == 0:
-            link(
-                block(g, ACROSS_X, 0, c), block(g, DIAGONAL, 0, c), at_y, (g, "d", c), (g, "gather")
-            )
-        to_core(g, ACROSS_X, c)
-        arrive((g, "y", c), block(g, ACROSS_Y, 0, c))
-        if c % 2 == 1:
-            link(
-                block(g, ACROSS_Y, 0, c), block(g, DIAGONAL, 0, c), at_x, (g, "d", c), (g, "gather")
-            )
-        to_core(g, ACROSS_Y, c)
+        for role, name, other, i in ((ACROSS_X, "x", at_y, c), (ACROSS_Y, "y", at_x, c ^ 1)):
+            arrive((g, name, i), block(g, role, 0, i))
+            if c % 2 == 0:
+                link(block(g, role, 0, i), block(g, DIAGONAL, 0, i), other, (g, "d", i), (g, "gather"))
+            to_core(g, role, i)
 
     def relay_diagonal(g, c):
         arrive((g, "d", c), block(g, DIAGONAL, 0, c))
@@ -245,7 +246,7 @@
             )
         return columns
 
-    def expert(g, role, between=lambda: None):
+    def expert(g, role):
         arrive((g, "core", role), tok[g].at[2 * role + 1])
         n = count[g]
         tokens_in = tok[g][2 * role : 2 * role + 2].reshape(2 * n, features)
@@ -258,7 +259,6 @@
             upward = jnp.dot(tokens_in, up_w[:, cols], preferred_element_type=jnp.float32) * scale
             hidden[: 2 * n, cols] = (gate / (1.0 + jnp.exp(-gate)) * upward).astype(jnp.bfloat16)
         inner = hidden[: 2 * n]
-        between()
         here, there = weight(g, role)
         for j in range(features // 256):
             cols = pl.ds(j * 256, 256)
@@ -302,15 +302,15 @@
             value = summed(g, ACROSS_Y, lo, hi)
             post(g, 1, landed[g].at[1], lo, hi, value, at_y, ("direct",))
 
-    def send_merged(g):
-        for p, (lo, hi) in enumerate(cuts(g)):
-            arrive((g, "across", 0, p), via[g].at[pl.ds(lo, hi - lo)])
-            value = summed(g, ACROSS_Y, lo, hi) + via[g][lo:hi].astype(jnp.float32)
-            post(g, 1, landed[g].at[1], lo, hi, value, at_y, ("merged", p))
-            lo, hi = lo + half[g], hi + half[g]
-            arrive((g, "across", 1, p), via[g].at[pl.ds(lo, hi - lo)])
-            value = summed(g, ACROSS_X, lo, hi) + via[g][lo:hi].astype(jnp.float32)
-            post(g, 0, landed[g].at[0], lo, hi, value, at_x, ("merged", p))
+    def send_merged(g, p):
+        lo, hi = cuts(g)[p]
+        arrive((g, "across", 0, p), via[g].at[pl.ds(lo, hi - lo)])
+        value = summed(g, ACROSS_Y, lo, hi) + via[g][lo:hi].astype(jnp.float32)
+        post(g, 1, landed[g].at[1], lo, hi, value, at_y, ("merged", p))
+        lo, hi = lo + half[g], hi + half[g]
+        arrive((g, "across", 1, p), via[g].at[pl.ds(lo, hi - lo)])
+        value = summed(g, ACROSS_X, lo, hi) + via[g][lo:hi].astype(jnp.float32)
+        post(g, 0, landed[g].at[0], lo, hi, value, at_x, ("merged", p))
 
     def finish(g):
         swapped(g, OWN)
@@ -330,64 +330,70 @@
                     cut = pl.ds(lo + first_row[g], hi - lo)
                     link(done_early.at[pl.ds(lo, hi - lo)], out_ref.at[0, cut], ahead, "home", "home")
 
-    def near():
-        meta_second(EARLY)
-        meta_arrive(EARLY, "near", 3)
+    def hopped(c):
+        arrive(("hop", c), block(LATE, OWN, 0, c))
+        share(LATE, c)
 
     meta_first(LATE)
-    for c in range(chunks[LATE]):
+    for c in range(chunks):
         link(incoming.at[0, part[LATE][c]], block(LATE, OWN, 0, c), ahead, ("hop", c), "hop")
-    for c in range(chunks[EARLY] - 1):
-        share(EARLY, c)
-    for copy in loads:
-        copy.start()
-    pl.semaphore_wait(hello, 1)
-    meta_link_back = (meta.at[meta_slot(LATE, 0)], meta.at[meta_slot(EARLY, 0)])
-    link(*meta_link_back, behind, (EARLY, "meta", "own"), "meta")
-    share(EARLY, chunks[EARLY] - 1)
+    for c in range(chunks):
+        share_x(EARLY, c)
+        share_y(EARLY, c ^ 1)
+        if c == chunks // 2:
+            for copy in loads:
+                copy.start()
+            pl.semaphore_wait(hello, 1)
+            meta_link_back = (meta.at[meta_slot(LATE, 0)], meta.at[meta_slot(EARLY, 0)])
+            link(*meta_link_back, behind, (EARLY, "meta", "own"), "meta")
     meta_arrive(LATE, "x")
     meta_arrive(LATE, "y")
     meta_second(LATE)
-    lag = chunks[EARLY] // 2
-    for c in range(max(chunks[EARLY], chunks[LATE] + lag)):
-        if c == lag:
-            meta_arrive(EARLY, "own")
-            meta_first(EARLY)
-            meta_link(EARLY, 0, 6, across, "d")
-        if c < chunks[EARLY]:
-            relay(EARLY, c)
-        if 0 <= c - lag < chunks[LATE]:
-            arrive(("hop", c - lag), block(LATE, OWN, 0, c - lag))
-            share(LATE, c - lag)
+    relay(EARLY, 0)
+    relay(EARLY, 1)
+    meta_arrive(EARLY, "own")
+    meta_first(EARLY)
+    meta_link(EARLY, 0, 6, across, "d")
+    relay(EARLY, 2)
+    hopped(0)
+    hopped(1)
+    relay(EARLY, 3)
+    meta_second(EARLY)
+    hopped(2)
+    hopped(3)
     meta_third(LATE)
     for copy in loads:
         copy.wait()
-    expert(EARLY, ACROSS_X, near)
+    meta_arrive(EARLY, "near", 3)
+    expert(EARLY, ACROSS_X)
     meta_third(EARLY)
+    for c in range(chunks):
+        relay_diagonal(EARLY, c)
     expert(EARLY, ACROSS_Y)
-    for c in range(chunks[EARLY]):
-        relay_diagonal(EARLY, c)
     relay(LATE, 0)
     meta_arrive(EARLY, "far")
     expert(EARLY, DIAGONAL)
-    for c in range(1, chunks[LATE]):
-        relay(LATE, c)
+    relay(LATE, 1)
+    relay(LATE, 2)
     send_diagonal(EARLY)
     send_direct(EARLY)
     expert(EARLY, OWN)
+    relay(LATE, 3)
     meta_arrive(LATE, "near", 3)
     meta_arrive(LATE, "far")
+    expert(LATE, OWN)
     expert(LATE, ACROSS_X)
-    for c in range(chunks[LATE]):
+    for c in range(chunks):
         relay_diagonal(LATE, c)
     expert(LATE, ACROSS_Y)
+    send_merged(EARLY, 0)
     expert(LATE, DIAGONAL)
-    send_merged(EARLY)
+    send_merged(EARLY, 1)
     send_diagonal(LATE)
     send_direct(LATE)
-    expert(LATE, OWN)
     finish(EARLY)
-    send_merged(LATE)
+    send_merged(LATE, 0)
+    send_merged(LATE, 1)
     finish(LATE)
     arrive("home", tok_early.at[0])
     left("hop", tok_late.at[0])
@@ -404,10 +410,10 @@
     n_pp, n_tp, n_ep = (lax.axis_size(a) for a in ("pp", "tp", "ep"))
     early = rows // 2
     groups = (early, rows - early)
-    chunks, pieces = (4, 4), 2
+    chunks, pieces = 4, 2
     hbm, vmem = pl.BlockSpec(memory_space=pl.ANY), pl.BlockSpec(memory_space=pltpu.VMEM)
     narrow = functools.partial(pltpu.VMEM, dtype=jnp.bfloat16)
-    arrivals = 3 * sum(chunks) + 8 + 8 + 2 * (3 * pieces + 1) + 1 + chunks[1] + 11
+    arrivals = 7 * chunks + 8 + 8 + 2 * (3 * pieces + 1) + 1 + 11
 
     def pair(*lead):
         return [narrow((*lead, n, features)) for n in groups]

time: 43.2 us -> 42.2 us (0.977)
  Pallas kernels: 42.2 us -> 41.2 us
    pallas_call x1, Pallas kernels: 42.2 us -> 41.2 us  [fused(): pl.pallas_call(functools.partial(exchange_kernel, (n_pp, n_tp, n_ep, top,...]
where the time goes in v4:
time: 42.2 us; the launch traced here: 42 us
  Pallas kernels  41.2 us (98%)
  local copies, waits for them, and re-layouts  0.8 us (2%)
    pallas_call x1, Pallas kernels, fused(): pl.pallas_call(functools.partial(exchange_kernel, (n_pp, n_tp, n_ep, top,...  41.2 us

profile of v4, /device:TPU:0, one launch (start us, length us, event | category | flops | bytes accessed | tf_op | source)
XLA Modules:
  0.0 42.0 jit_solution(17164581105673995599)
XLA Ops:
  0.0 41.2 %shard_map.64 = bf16[1,128,2048]{2,1,0:T(8,128)(2,1)S(1)} custom-call(bf16[1,128,2048]{2,1,0:T(8,128)(2,1)} %incoming.1, s32[2,128]{1,0:T(2,128)} %bitcast.6, f32[2,128]{1,0:T(2,128)} %bitcast.7, bf16[1,2048,768]{2,1,0:T(8,128)(2,1)} %gate_hbm.1, bf16[1,2048,768]{2,1,0:T(8,128)(2,1)} %up_hbm.1, bf16[1,768,2048]{2,1,0:T(8,128)(2,1)} %down_hbm.1), custom_call_target="tpu_custom_call" | custom-call | tf_op jit(solution)/shard_map/pallas_call | solution.py:421
  41.2 0.8 %copy.8 = bf16[1,128,2048]{2,1,0:T(8,128)(2,1)} copy(bf16[1,128,2048]{2,1,0:T(8,128)(2,1)S(1)} %shard_map.64) | data formatting | bytes 1048576

commit v5 on v4

--- a/solution.py
+++ b/solution.py
@@ -180,11 +180,11 @@
         return tok[g].at[2 * role + side, part[g][c]]
 
     def share_x(g, c):
-        link(block(g, OWN, 0, c), block(g, ACROSS_X, 0, c), at_x, (g, "x", c), (g, "gather"))
+        link(block(g, OWN, 0, c), block(g, ACROSS_X, 0, c), at_x, (g, "plane", c), (g, "gather"))
         to_core(g, OWN, c)
 
     def share_y(g, c):
-        link(block(g, OWN, 0, c), block(g, ACROSS_Y, 0, c), at_y, (g, "y", c), (g, "gather"))
+        link(block(g, OWN, 0, c), block(g, ACROSS_Y, 0, c), at_y, (g, "plane", c ^ 1), (g, "gather"))
 
     def share(g, c):
         share_x(g, c)
@@ -196,15 +196,16 @@
         link(block(g, role, 0, c), block(g, role, 1, c), at_core, (g, "core", role), (g, "gather"))
 
     def relay(g, c):
-        for role, name, other, i in ((ACROSS_X, "x", at_y, c), (ACROSS_Y, "y", at_x, c ^ 1)):
-            arrive((g, name, i), block(g, role, 0, i))
+        arrive((g, "plane", c), tok[g].at[0, pl.ds(0, 2 * (count[g] // chunks))])
+        for role, other, i in ((ACROSS_X, at_y, c), (ACROSS_Y, at_x, c ^ 1)):
             if c % 2 == 0:
-                link(block(g, role, 0, i), block(g, DIAGONAL, 0, i), other, (g, "d", i), (g, "gather"))
+                link(block(g, role, 0, i), block(g, DIAGONAL, 0, i), other, (g, "d"), (g, "gather"))
             to_core(g, role, i)
 
-    def relay_diagonal(g, c):
-        arrive((g, "d", c), block(g, DIAGONAL, 0, c))
-        to_core(g, DIAGONAL, c)
+    def relay_diagonal(g):
+        there, here = (tok[g].at[2 * DIAGONAL + side] for side in (1, 0))
+        arrive((g, "d"), here)
+        link(here, there, at_core, (g, "core", DIAGONAL), (g, "gather"))
 
     def meta_link(g, src, dst, peer, name):
         src, dst = meta_slot(g, src), meta_slot(g, dst)
@@ -214,22 +215,21 @@
         arrive((g, "meta", name), meta.at[pl.ds(0, n)])
 
     def meta_first(g):
-        meta_link(g, 0, 2, at_x, "x")
-        meta_link(g, 0, 4, at_y, "y")
+        meta_link(g, 0, 2, at_x, "plane")
+        meta_link(g, 0, 4, at_y, "plane")
         meta_link(g, 0, 1, at_core, "near")
 
     def meta_second(g):
         if g == LATE:
             meta_link(g, 2, 6, at_y, "d")
         else:
-            meta_arrive(g, "x")
-            meta_arrive(g, "y")
+            meta_arrive(g, "plane", 2)
         meta_link(g, 2, 3, at_core, "near")
         meta_link(g, 4, 5, at_core, "near")
 
     def meta_third(g):
         meta_arrive(g, "d")
-        meta_link(g, 6, 7, at_core, "far")
+        meta_link(g, 6, 7, at_core, "far" if g == EARLY else "near")
 
     mine = (tp * n_ep + ep).astype(jnp.float32)
 
@@ -287,10 +287,10 @@
         swapped(g, DIAGONAL)
         for p, (lo, hi) in enumerate(cuts(g)):
             value = summed(g, DIAGONAL, lo, hi)
-            post(g, 2, via[g], lo, hi, value, at_x, ("across", 0, p))
+            post(g, 2, via[g], lo, hi, value, at_x, ("across", p))
             lo, hi = lo + half[g], hi + half[g]
             value = summed(g, DIAGONAL, lo, hi)
-            post(g, 2, via[g], lo, hi, value, at_y, ("across", 1, p))
+            post(g, 2, via[g], lo, hi, value, at_y, ("across", p))
 
     def send_direct(g):
         swapped(g, ACROSS_X)
@@ -304,11 +304,10 @@
 
     def send_merged(g, p):
         lo, hi = cuts(g)[p]
-        arrive((g, "across", 0, p), via[g].at[pl.ds(lo, hi - lo)])
+        arrive((g, "across", p), via[g].at[pl.ds(0, 2 * (hi - lo))])
         value = summed(g, ACROSS_Y, lo, hi) + via[g][lo:hi].astype(jnp.float32)
         post(g, 1, landed[g].at[1], lo, hi, value, at_y, ("merged", p))
         lo, hi = lo + half[g], hi + half[g]
-        arrive((g, "across", 1, p), via[g].at[pl.ds(lo, hi - lo)])
         value = summed(g, ACROSS_X, lo, hi) + via[g][lo:hi].astype(jnp.float32)
         post(g, 0, landed[g].at[0], lo, hi, value, at_x, ("merged", p))
 
@@ -346,8 +345,7 @@
             pl.semaphore_wait(hello, 1)
             meta_link_back = (meta.at[meta_slot(LATE, 0)], meta.at[meta_slot(EARLY, 0)])
             link(*meta_link_back, behind, (EARLY, "meta", "own"), "meta")
-    meta_arrive(LATE, "x")
-    meta_arrive(LATE, "y")
+    meta_arrive(LATE, "plane", 2)
     meta_second(LATE)
     relay(EARLY, 0)
     relay(EARLY, 1)
@@ -367,8 +365,7 @@
     meta_arrive(EARLY, "near", 3)
     expert(EARLY, ACROSS_X)
     meta_third(EARLY)
-    for c in range(chunks):
-        relay_diagonal(EARLY, c)
+    relay_diagonal(EARLY)
     expert(EARLY, ACROSS_Y)
     relay(LATE, 0)
     meta_arrive(EARLY, "far")
@@ -377,20 +374,18 @@
     relay(LATE, 2)
     send_diagonal(EARLY)
     send_direct(EARLY)
+    relay(LATE, 3)
     expert(EARLY, OWN)
-    relay(LATE, 3)
-    meta_arrive(LATE, "near", 3)
-    meta_arrive(LATE, "far")
-    expert(LATE, OWN)
+    meta_arrive(LATE, "near", 4)
     expert(LATE, ACROSS_X)
-    for c in range(chunks):
-        relay_diagonal(LATE, c)
+    relay_diagonal(LATE)
     expert(LATE, ACROSS_Y)
     send_merged(EARLY, 0)
     expert(LATE, DIAGONAL)
     send_merged(EARLY, 1)
     send_diagonal(LATE)
     send_direct(LATE)
+    expert(LATE, OWN)
     finish(EARLY)
     send_merged(LATE, 0)
     send_merged(LATE, 1)
@@ -413,7 +408,7 @@
     chunks, pieces = 4, 2
     hbm, vmem = pl.BlockSpec(memory_space=pl.ANY), pl.BlockSpec(memory_space=pltpu.VMEM)
     narrow = functools.partial(pltpu.VMEM, dtype=jnp.bfloat16)
-    arrivals = 7 * chunks + 8 + 8 + 2 * (3 * pieces + 1) + 1 + 11
+    arrivals = 3 * chunks + 2 * (1 + 4 + 4 + 2 * pieces + 1) + 1 + 8
 
     def pair(*lead):
         return [narrow((*lead, n, features)) for n in groups]

time: 42.2 us -> 41.2 us (0.976)
  Pallas kernels: 41.2 us -> 40.3 us
    pallas_call x1, Pallas kernels: 41.2 us -> 40.3 us  [fused(): pl.pallas_call(functools.partial(exchange_kernel, (n_pp, n_tp, n_ep, top,...]
where the time goes in v5:
time: 41.2 us; the launch traced here: 41.1 us
  Pallas kernels  40.3 us (98%)
  local copies, waits for them, and re-layouts  0.8 us (2%)
    pallas_call x1, Pallas kernels, fused(): pl.pallas_call(functools.partial(exchange_kernel, (n_pp, n_tp, n_ep, top,...  40.3 us

profile of v5, /device:TPU:0, one launch (start us, length us, event | category | flops | bytes accessed | tf_op | source)
XLA Modules:
  0.0 41.1 jit_solution(16616205426417838823)
XLA Ops:
  0.0 40.3 %shard_map.64 = bf16[1,128,2048]{2,1,0:T(8,128)(2,1)S(1)} custom-call(bf16[1,128,2048]{2,1,0:T(8,128)(2,1)} %incoming.1, s32[2,128]{1,0:T(2,128)} %bitcast.6, f32[2,128]{1,0:T(2,128)} %bitcast.7, bf16[1,2048,768]{2,1,0:T(8,128)(2,1)} %gate_hbm.1, bf16[1,2048,768]{2,1,0:T(8,128)(2,1)} %up_hbm.1, bf16[1,768,2048]{2,1,0:T(8,128)(2,1)} %down_hbm.1), custom_call_target="tpu_custom_call" | custom-call | tf_op jit(solution)/shard_map/pallas_call | solution.py:416
  40.3 0.8 %copy.8 = bf16[1,128,2048]{2,1,0:T(8,128)(2,1)} copy(bf16[1,128,2048]{2,1,0:T(8,128)(2,1)S(1)} %shard_map.64) | data formatting | bytes 1048576

commit v6 on v5

--- a/solution.py
+++ b/solution.py
@@ -101,12 +101,16 @@
     via_early,
     via_late,
     done_early,
+    lent_early,
+    lent_late,
+    sum_early,
+    sum_late,
     send_sem,
     recv_sem,
     load_sem,
     hello,
 ):
-    n_pp, n_tp, n_ep, top, chunks, pieces = sizes
+    n_pp, n_tp, n_ep, top, chunks, pieces, lend = sizes
     features, ff = gate_w.shape
     pp, tp, ep = lax.axis_index("pp"), lax.axis_index("tp"), lax.axis_index("ep")
     other_core = tp + 1 - 2 * (tp % 2)
@@ -114,6 +118,8 @@
     at_y = {"tp": (tp + 2) % n_tp}
     at_core = {"tp": other_core}
     across = {"ep": (ep + 1) % n_ep, "tp": (tp + 2) % n_tp}
+    far_x, far_y = {**at_x, **at_core}, {"tp": (other_core + 2) % n_tp}
+    inner_core, outer_core = tp % 2 == 0, tp % 2 == 1
     ahead, behind = {"pp": (pp + 1) % n_pp}, {"pp": (pp + n_pp - 1) % n_pp}
 
     tok = (tok_early, tok_late)
@@ -123,6 +129,8 @@
     count = [t.shape[1] for t in tok]
     first_row = [count[LATE], 0]
     half = [n // 2 for n in count]
+    lent, lent_sum = (lent_early, lent_late), (sum_early, sum_late)
+    lent_rows = [h // p * m for h, p, m in zip(half, pieces, lend)]
     part = [[pl.ds(c * (n // chunks), n // chunks) for c in range(chunks)] for n in count]
 
     loads = []
@@ -267,6 +275,13 @@
             kept[g][role, :, cols] = (y[:n] * here).astype(jnp.bfloat16)
             passed[g][role, :, cols] = (y[n:] * there).astype(jnp.bfloat16)
         link(passed[g].at[role], partner[g].at[role], at_core, (g, "swap", role), (g, "return"))
+        if role in (ACROSS_X, ACROSS_Y):
+            k = (ACROSS_X, ACROSS_Y).index(role)
+
+            @pl.when(inner_core)
+            def _():
+                rows = pl.ds(k * half[g], lent_rows[g])
+                link(kept[g].at[role, rows], lent[g].at[k], at_core, (g, "lent"), (g, "lent"))
 
     def swapped(g, role):
         arrive((g, "swap", role), partner[g].at[role])
@@ -275,13 +290,13 @@
         return kept[g][role, lo:hi].astype(jnp.float32) + partner[g][role, lo:hi].astype(jnp.float32)
 
     def cuts(g):
-        size = half[g] // pieces
-        return [(p * size, (p + 1) * size) for p in range(pieces)]
-
-    def post(g, buffer, landing, lo, hi, value, peer, arrives):
+        size = half[g] // pieces[g]
+        return [(p * size, (p + 1) * size) for p in range(pieces[g])]
+
+    def post(g, buffer, landing, lo, hi, value, peer, arrives, leaves="return"):
         to[g][buffer, lo:hi] = value.astype(jnp.bfloat16)
         rows = pl.ds(lo, hi - lo)
-        link(to[g].at[buffer, rows], landing.at[rows], peer, (g, *arrives), (g, "return"))
+        link(to[g].at[buffer, rows], landing.at[rows], peer, (g, *arrives), (g, leaves))
 
     def send_diagonal(g):
         swapped(g, DIAGONAL)
@@ -295,12 +310,32 @@
     def send_direct(g):
         swapped(g, ACROSS_X)
         swapped(g, ACROSS_Y)
-        for lo, hi in cuts(g):
-            value = summed(g, ACROSS_X, lo, hi)
-            post(g, 0, landed[g].at[0], lo, hi, value, at_x, ("direct",))
-            lo, hi = lo + half[g], hi + half[g]
-            value = summed(g, ACROSS_Y, lo, hi)
-            post(g, 1, landed[g].at[1], lo, hi, value, at_y, ("direct",))
+
+        @pl.when(outer_core)
+        def _():
+            send_lent(g)
+            for p in range(lend[g]):
+                send_own(g, p, "outer")
+
+        for p in range(lend[g], pieces[g]):
+            send_own(g, p, "both")
+
+    def send_own(g, p, leaves):
+        for k, role, peer in ((0, ACROSS_X, at_x), (1, ACROSS_Y, at_y)):
+            lo, hi = (edge + k * half[g] for edge in cuts(g)[p])
+            value = summed(g, role, lo, hi)
+            post(g, k, landed[g].at[k], lo, hi, value, peer, ("direct",), leaves)
+
+    def send_lent(g):
+        arrive((g, "lent"), via[g].at[pl.ds(0, 2 * lent_rows[g])])
+        for k, role, peer in ((0, ACROSS_X, far_x), (1, ACROSS_Y, far_y)):
+            for lo, hi in cuts(g)[: lend[g]]:
+                rows = pl.ds(k * half[g] + lo, hi - lo)
+                value = lent[g][k, lo:hi].astype(jnp.float32)
+                value += passed[g][role, rows].astype(jnp.float32)
+                lent_sum[g][k, lo:hi] = value.astype(jnp.bfloat16)
+                source = lent_sum[g].at[k, pl.ds(lo, hi - lo)]
+                link(source, landed[g].at[k, rows], peer, (g, "direct"), (g, "lent"))
 
     def send_merged(g, p):
         lo, hi = cuts(g)[p]
@@ -380,22 +415,33 @@
     expert(LATE, ACROSS_X)
     relay_diagonal(LATE)
     expert(LATE, ACROSS_Y)
-    send_merged(EARLY, 0)
+    for p in range(max(1, pieces[EARLY] // 2)):
+        send_merged(EARLY, p)
     expert(LATE, DIAGONAL)
-    send_merged(EARLY, 1)
+    for p in range(max(1, pieces[EARLY] // 2), pieces[EARLY]):
+        send_merged(EARLY, p)
     send_diagonal(LATE)
     send_direct(LATE)
+    finish(EARLY)
     expert(LATE, OWN)
-    finish(EARLY)
-    send_merged(LATE, 0)
-    send_merged(LATE, 1)
+    for p in range(pieces[LATE]):
+        send_merged(LATE, p)
     finish(LATE)
     arrive("home", tok_early.at[0])
     left("hop", tok_late.at[0])
     left("home", tok_early.at[0])
     for g in (EARLY, LATE):
         left((g, "gather"), tok[g].at[pl.ds(0, 7)])
-        left((g, "return"), tok[g].at[pl.ds(0, 7)])
+        left((g, "return"), tok[g].at[pl.ds(0, 6)])
+        left((g, "lent"), via[g].at[pl.ds(0, 2 * lent_rows[g])])
+        if lend[g] < pieces[g]:
+            left((g, "both"), via[g].at[pl.ds(0, count[g] - 2 * lent_rows[g])])
+
+    @pl.when(outer_core)
+    def _():
+        for g in (EARLY, LATE):
+            left((g, "outer"), via[g].at[pl.ds(0, 2 * lent_rows[g])])
+
     left("meta", meta.at[pl.ds(0, 15)])
 
 
@@ -405,16 +451,16 @@
     n_pp, n_tp, n_ep = (lax.axis_size(a) for a in ("pp", "tp", "ep"))
     early = rows // 2
     groups = (early, rows - early)
-    chunks, pieces = 4, 2
+    chunks, pieces, lend = 4, (2, 2), (2, 1)
     hbm, vmem = pl.BlockSpec(memory_space=pl.ANY), pl.BlockSpec(memory_space=pltpu.VMEM)
     narrow = functools.partial(pltpu.VMEM, dtype=jnp.bfloat16)
-    arrivals = 3 * chunks + 2 * (1 + 4 + 4 + 2 * pieces + 1) + 1 + 8
+    arrivals = 3 * chunks + 2 * (1 + 4 + 4 + 1 + sum(pieces)) + 3 + 8
 
     def pair(*lead):
         return [narrow((*lead, n, features)) for n in groups]
 
     return pl.pallas_call(
-        functools.partial(exchange_kernel, (n_pp, n_tp, n_ep, top, chunks, pieces)),
+        functools.partial(exchange_kernel, (n_pp, n_tp, n_ep, top, chunks, pieces, lend)),
         out_shape=pltpu.VMEM(incoming.shape, incoming.dtype),
         in_specs=[hbm] * 6,
         out_specs=vmem,
@@ -434,7 +480,8 @@
             *pair(2),
             *pair(),
             narrow((early, features)),
-            pltpu.SemaphoreType.DMA((7,)),
+            *[narrow((2, n // 2 // p * m, features)) for n, p, m in zip(groups, pieces, lend)] * 2,
+            pltpu.SemaphoreType.DMA((11 + sum(m < p for m, p in zip(lend, pieces)),)),
             pltpu.SemaphoreType.DMA((arrivals,)),
             pltpu.SemaphoreType.DMA((6,)),
             pltpu.SemaphoreType.REGULAR,

time: 41.2 us -> 40.6 us (0.985)
  Pallas kernels: 40.3 us -> 39.6 us
    pallas_call x1, Pallas kernels: 40.3 us -> 39.6 us  [fused(): pl.pallas_call(functools.partial(exchange_kernel, (n_pp, n_tp, n_ep, top,...]
where the time goes in v6:
time: 40.6 us; the launch traced here: 40.4 us
  Pallas kernels  39.6 us (98%)
  local copies, waits for them, and re-layouts  0.8 us (2%)
    pallas_call x1, Pallas kernels, fused(): pl.pallas_call(functools.partial(exchange_kernel, (n_pp, n_tp, n_ep, top,...  39.6 us

profile of v6, /device:TPU:0, one launch (start us, length us, event | category | flops | bytes accessed | tf_op | source)
XLA Modules:
  0.0 40.4 jit_solution(5564897499225579808)
XLA Ops:
  0.0 39.6 %shard_map.64 = bf16[1,128,2048]{2,1,0:T(8,128)(2,1)S(1)} custom-call(bf16[1,128,2048]{2,1,0:T(8,128)(2,1)} %incoming.1, s32[2,128]{1,0:T(2,128)} %bitcast.6, f32[2,128]{1,0:T(2,128)} %bitcast.7, bf16[1,2048,768]{2,1,0:T(8,128)(2,1)} %gate_hbm.1, bf16[1,2048,768]{2,1,0:T(8,128)(2,1)} %up_hbm.1, bf16[1,768,2048]{2,1,0:T(8,128)(2,1)} %down_hbm.1), custom_call_target="tpu_custom_call" | custom-call | tf_op jit(solution)/shard_map/pallas_call | solution.py:462
  39.6 0.8 %copy.8 = bf16[1,128,2048]{2,1,0:T(8,128)(2,1)} copy(bf16[1,128,2048]{2,1,0:T(8,128)(2,1)S(1)} %shard_map.64) | data formatting | bytes 1048576
